TPU v7x, 16 devices: a whole 2x2x2 slice. The times are simulated.
16 devices in a mesh: pp: 2 (over z), tp: 8 (over y, x, core).
Axes of the slice: x: 2, y: 2, z: 2, core: 2. Of those that a mesh axis runs over, the one named last changes fastest.
Arguments:
- activations: bfloat16 [384, 28, 28, 384], P(('pp', 'tp'))
- conv_w: bfloat16 [3, 3, 384, 384], P(None, None, 'tp')
- bn_scale: float32 [384], P('tp')
- bn_shift: float32 [384], P('tp')
Outputs:
- output: bfloat16 [384, 28, 28, 384], P('pp', None, None, 'tp')
All inputs are finite; a program needn't handle non-finite values.
Results may differ from a plain program's by a relative error of at most 0.001.
Values are sent between devices in bfloat16 or wider.
A program may use at most 1 GiB of HBM per device.

v0:
```python
import jax
import jax.numpy as jnp
from jax import lax
from jax.sharding import PartitionSpec as P

CONV_DIMS = ("NHWC", "HWIO", "NHWC")


def solution(mesh):
    half_pp = mesh.shape["pp"] // 2
    send_pairs = [(source, source + half_pp) for source in range(half_pp)]

    def local_step(act_block, w_shard, scale_shard, shift_shard):
        by_channel = lax.all_to_all(act_block, "tp", 3, 0, tiled=True)
        moved_in = lax.ppermute(by_channel, "pp", perm=send_pairs)
        partial_sum = lax.conv_general_dilated(moved_in, w_shard, (1, 1), "SAME", dimension_numbers=CONV_DIMS, preferred_element_type=jnp.float32)
        pre_act = lax.psum_scatter(partial_sum, "tp", scatter_dimension=3, tiled=True)
        y_val = pre_act * scale_shard + shift_shard
        stage_mask = (lax.axis_index("pp") >= half_pp).astype(jnp.float32)
        return (jnp.maximum(y_val, 0.0) * stage_mask).astype(jnp.bfloat16)

    return jax.shard_map(local_step, mesh=mesh, in_specs=(P(("pp", "tp")), P(None, None, "tp", None), P("tp"), P("tp")), out_specs=P("pp", None, None, "tp"), check_vma=False)
```

profile of v0, /device:TPU:0, one launch (start us, length us, event | category | flops | bytes accessed | tf_op | source)
XLA Modules:
  0.0 3022.1 jit_solution(9389701632237665253)
XLA Ops:
  6.5 0.0 copy-start
  6.5 0.0 reduce-scatter.2.cloned.1.call-start
  6.5 100.8 %copy.11 = bf16[24,28,28,384]{2,0,1,3:T(8,128)(2,1)} copy(bf16[24,28,28,384]{3,0,2,1:T(8,128)(2,1)} %param.4) | data formatting | bytes 28901376 | tf_op args[0]
  107.3 206.8 %reshape.2 = bf16[8,2,451584]{2,1,0:T(2,128)(2,1)} reshape(bf16[384,28,24,28]{3,2,1,0:T(8,128)(2,1)} %bitcast.9) | data formatting | bytes 28901376
  314.1 166.9 %all_to_all.18 = bf16[8,2,451584]{2,1,0:T(2,128)(2,1)} all-to-all(bf16[8,2,451584]{2,1,0:T(2,128)(2,1)} %reshape.2), channel_id=1, replica_groups=mesh['pp'=2,'tp'=8] {'tp'}, dimensions={0} | all-to-all | bytes 28901376 | tf_op jit(solution)/shard_map/all_to_all | solution.py:14
  481.0 222.5 %reshape.3 = bf16[384,28,24,28]{3,2,1,0:T(8,128)(2,1)} reshape(bf16[8,2,451584]{2,1,0:T(2,128)(2,1)} %all_to_all.18) | data formatting | bytes 28901376
  703.5 85.6 %copy.12 = bf16[24,28,28,8,48]{4,0,3,2,1:T(8,128)(2,1)} copy(bf16[24,28,28,8,48]{2,0,1,4,3:T(8,128)(2,1)} %bitcast.8) | data formatting | bytes 28901376 | tf_op jit(solution)/shard_map/all_to_all | solution.py:14
  789.1 38.7 %copy.13 = bf16[192,28,28,48]{0,3,2,1:T(8,128)(2,1)} copy(bf16[192,28,28,48]{3,0,2,1:T(8,128)(2,1)} %bitcast.10) | data formatting | bytes 28901376 | tf_op jit(solution)/shard_map/all_to_all | solution.py:14
  827.8 10.7 collective-permute-start
  838.5 406.5 %collective-permute-done = bf16[192,28,28,48]{0,3,2,1:T(8,128)(2,1)} collective-permute-done((bf16[192,28,28,48]{0,3,2,1:T(8,128)(2,1)}, bf16[192,28,28,48]{0,3,2,1:T(8,128)(2,1)}, u32[]{:S(2)}, u32[]{:S(2)}) %collective-permute-start) | collective-permute-done | bytes 14450720 | tf_op jit(solution)/shard_map/ppermute | solution.py:15
  1245.0 0.0 copy-done
  1245.0 110.7 %fusion = f32[192,28,28,384]{0,3,2,1:T(8,128)} fusion(bf16[192,28,28,48]{0,3,2,1:T(8,128)(2,1)} %collective-permute-done, bf16[3,3,48,384]{3,2,1,0:T(8,128)(2,1)S(1)} %copy-done), kind=kOutput, calls=%fused_computation.1 | convolution fusion | flops 47591718912 | bytes 245993472 | tf_op jit(solution)/shard_map/conv_general_dilated | solution.py:16
  1355.7 0.0 copy-start.2
  1355.7 0.0 copy-start.3
  1355.7 0.0 reduce-scatter.2.cloned.1.call-update
  1355.7 0.0 copy-start.1
  1355.8 1636.7 %reduce-scatter.2.cloned.1.call-done = f32[192,28,28,48]{0,3,2,1:T(8,128)} async-done(((f32[192,28,28,384]{0,3,2,1:T(8,128)}), f32[192,28,28,48]{0,3,2,1:T(8,128)}) %reduce-scatter.2.cloned.1.call-update) | async-done | bytes 28901392 | tf_op jit(solution)/shard_map/reduce_scatter | solution.py:17
  2992.5 0.0 copy-done.2
  2992.5 0.0 copy-done.3
  2992.5 22.5 multiply_convert_fusion
  3015.0 0.0 copy-done.1
Async XLA Ops:
  6.5 1238.5 %copy-start = (bf16[3,3,48,384]{3,2,1,0:T(8,128)(2,1)S(1)}, bf16[3,3,48,384]{3,2,1,0:T(8,128)(2,1)}, u32[]{:S(2)}) copy-start(bf16[3,3,48,384]{3,2,1,0:T(8,128)(2,1)} %param.5) | copy-start | bytes 995332
  6.5 2985.9 %reduce-scatter.2.cloned.1.call-start = ((), (), s32[]{:S(2)}) async-start(), calls=%async_computation.2 | async-start | bytes 346816512 | tf_op jit(solution)/shard_map/reduce_scatter | solution.py:17
  827.8 417.2 %collective-permute-start = (bf16[192,28,28,48]{0,3,2,1:T(8,128)(2,1)}, bf16[192,28,28,48]{0,3,2,1:T(8,128)(2,1)}, u32[]{:S(2)}, u32[]{:S(2)}) collective-permute-start(bf16[192,28,28,48]{0,3,2,1:T(8,128)(2,1)} %copy.13), channel_id=1, source_target_pairs={{0,8},{1,9},{2,10},{3,11},{4,12},{5,13},{6,14},{7,15}} | collective-permute-start | bytes 43352072 | tf_op jit(solution)/shard_map/ppermute | solution.py:15
  1355.7 1636.8 %copy-start.2 = (f32[48]{0:T(128)S(1)}, f32[48]{0:T(128)}, u32[]{:S(2)}) copy-start(f32[48]{0:T(128)} %param.7) | copy-start | bytes 580
  1355.7 1636.8 %copy-start.3 = (f32[48]{0:T(128)S(1)}, f32[48]{0:T(128)}, u32[]{:S(2)}) copy-start(f32[48]{0:T(128)} %param.6) | copy-start | bytes 580
  1355.7 1659.2 %copy-start.1 = (bf16[3,3,48,384]{3,2,1,0:T(8,128)(2,1)S(1)}, bf16[3,3,48,384]{3,2,1,0:T(8,128)(2,1)}, u32[]{:S(2)}) copy-start(bf16[3,3,48,384]{3,2,1,0:T(8,128)(2,1)} %param.5) | copy-start | bytes 995332
Sparse Core Ops, SparseCore 0:
  1355.9 1636.5 reduce-scatter.1
where the time goes:
time: 3030 us; the launch traced here: 3020 us
  waiting for transfers between devices  2040 us (67%)
  local copies, waits for them, and re-layouts  654 us (22%)
  blocking collectives  167 us (6%)
  matrix products  111 us (4%)
    reduce_scatter x1, waiting for transfers between devices, local_step(): lax.psum_scatter(partial_sum, 'tp', scatter_dimension=3, tiled=True)  1640 us
    unnamed x11, local copies, waits for them, and re-layouts  530 us
    ppermute x1, waiting for transfers between devices, local_step(): moved_in = lax.ppermute(by_channel, 'pp', perm=send_pairs)  407 us
    all_to_all x1, blocking collectives, local_step(): by_channel = lax.all_to_all(act_block, 'tp', 3, 0, tiled=True)  167 us
    all_to_all x2, local copies, waits for them, and re-layouts, local_step(): by_channel = lax.all_to_all(act_block, 'tp', 3, 0, tiled=True)  124 us
    conv_general_dilated x1, matrix products, local_step(): lax.conv_general_dilated(moved_in, w_shard, (1, 1), 'SAME', dimension_num...  111 us
  transfers between devices with their start and end apart: 2, of which 2 were waited for; matrix products, arithmetic and copies ran while one was open for 0% of the time, Pallas kernels for 0%

commit v1 on v0

v1 whole, which is shorter than its diff:
```python
import functools

import jax
import jax.numpy as jnp
from jax import lax
from jax.experimental import pallas as pl
from jax.experimental.pallas import tpu as pltpu
from jax.sharding import PartitionSpec as P


BF16 = jnp.bfloat16
F32 = jnp.float32
ROWS = 28
COLS = 28
CH = 384
BLK = 48
IMGS = 24
RAW = 8
LIVE = IMGS - RAW
LANES = 128
VMEM_LIMIT = 60 * 1024 * 1024
HEAD = 2
CROSS_CHUNKS = ((0, 16), (16, 12))
LOCAL_CHUNKS = (((0, 28), (28, 28)), ((56, 16), (72, 12), (84, 8), (92, 6)))


def conv_body(meta_ref, *refs, **sizes):
    @pl.when(meta_ref[2] == 1)
    def _():
        conv_step(meta_ref, refs, **sizes)


def conv_step(meta_ref, refs, row0, img0, imgs, step_rows, heights):
    outs = refs[-11:-3]
    pad, col, flip = refs[-3:]
    edge = jnp.zeros((imgs, CH), BF16)
    for j in range(step_rows + 2):
        row = step_rows * pl.program_id(0) + row0 - 1 + j

        @pl.when(jnp.logical_or(row < 0, row >= ROWS))
        def _():
            pad[j, 1 : COLS + 1] = jnp.zeros((COLS, imgs, CH), BF16)

        begin = 0
        for piece, height in enumerate(heights):
            row_ref = refs[piece * (step_rows + 2) + j]

            @pl.when(jnp.logical_and(row >= begin, row < begin + height))
            def _():
                pad[j, 1 : COLS + 1] = row_ref[0, :, img0 : img0 + imgs, :]

            begin += height
        pad[j, 0] = edge
        pad[j, COLS + 1] = edge
    w_ref, scale_ref, shift_ref = refs[len(heights) * (step_rows + 2) :][:3]
    size = step_rows * COLS * imgs
    for a in range(3):
        for b in range(3):
            tap = 3 * a + b
            col[:, tap * CH : (tap + 1) * CH] = pad[a : a + step_rows, b : b + COLS].reshape(size, CH)
    pre = jnp.dot(col[...], w_ref[...], preferred_element_type=F32)
    z_val = jnp.maximum(pre * scale_ref[...] + shift_ref[...], 0.0)
    for g in range(size // LANES):
        group = z_val[g * LANES : (g + 1) * LANES]
        if imgs == RAW:
            group = group.reshape(2, 8, 8, CH).swapaxes(0, 1).reshape(LANES, CH)
            turn = meta_ref[1]
        else:
            turn = meta_ref[1] + 8 * ((7 * (row0 // 2 + pl.program_id(0)) + g) % 2)
        flip[g] = pltpu.roll(group, turn, 0).astype(BF16).T
    for k in range(8):
        start = pl.multiple_of(lax.bitwise_xor(meta_ref[0], k) * BLK, BLK)
        for g in range(size // LANES):
            outs[k][g] = flip[g, pl.ds(start, BLK), :]


def conv_call(meta, pieces, w_full, scale, shift, after, row0, steps, img0, imgs, step_rows):
    size = step_rows * COLS * imgs
    groups = size // LANES

    def row_specs(begin, piece):
        height, _, depth, _ = piece.shape
        return [
            pl.BlockSpec((1, COLS, depth, CH), lambda i, m, j=j: (jnp.clip(step_rows * i * m[2] + row0 - 1 + j - begin, 0, height - 1), 0, 0, 0))
            for j in range(step_rows + 2)
        ]

    def whole(*shape):
        return pl.BlockSpec(shape, lambda i, m: (0,) * len(shape))

    heights = tuple(piece.shape[0] for piece in pieces)
    specs, operands, begin = [], [], 0
    for piece in pieces:
        specs += row_specs(begin, piece)
        operands += [piece] * (step_rows + 2)
        begin += piece.shape[0]
    return pl.pallas_call(
        functools.partial(conv_body, row0=row0, img0=img0, imgs=imgs, step_rows=step_rows, heights=heights),
        grid_spec=pltpu.PrefetchScalarGridSpec(
            num_scalar_prefetch=1,
            grid=(steps,),
            in_specs=specs + [whole(9 * CH, CH), whole(1, CH), whole(1, CH)] + [pl.BlockSpec(memory_space=pl.ANY)] * len(after),
            out_specs=[pl.BlockSpec((groups, BLK, LANES), lambda i, m: (i * m[2], 0, 0))] * 8,
            scratch_shapes=[
                pltpu.VMEM((step_rows + 2, COLS + 2, imgs, CH), BF16),
                pltpu.VMEM((size, 9 * CH), BF16),
                pltpu.VMEM((groups, CH, LANES), BF16),
            ],
        ),
        out_shape=[jax.ShapeDtypeStruct((steps * groups, BLK, LANES), BF16)] * 8,
        compiler_params=pltpu.CompilerParams(vmem_limit_bytes=VMEM_LIMIT),
        cost_estimate=pl.CostEstimate(flops=2 * steps * size * 9 * CH * CH, bytes_accessed=steps * size * CH * 4, transcendentals=0),
    )(meta, *operands, w_full, scale, shift, *after)


def turned_slot(turn):
    lane = lax.broadcasted_iota(jnp.int32, (16, LANES), 1)
    return ((lane // 8 - turn) & 15).astype(F32).astype(BF16)


def merge_body(meta_ref, *refs, aliased):
    z_refs, r_refs = refs[0:6], refs[6:14]
    out = refs[15] if aliased else refs[14]
    z_hold, r_hold = refs[-2:]
    slots = ([], [])
    for d in range(8):
        for hold, some in ((r_hold, (3 * d,)), (z_hold, (3 * d + 1, 3 * d + 2))):
            for tile in range(2):
                inside = [s - 16 * tile for s in some if 16 * tile <= s < 16 * tile + 16]
                if inside:
                    slots[tile].append((hold, d, inside[0], len(inside)))

    def merge_pixels(p, odd):
        turn = 2 * p + odd
        slot = turned_slot(turn)
        masks = []
        for tile in range(2):
            for hold, d, begin, count in slots[tile]:
                mask = slot == begin if count == 1 else jnp.logical_and(slot >= begin, slot <= begin + 1)
                masks.append(mask)
        for r in range(7):
            g = 2 * r + odd
            for row in range(0, BLK, 16):
                at = 0
                for tile in range(2):
                    value = None
                    for hold, d, begin, count in slots[tile]:
                        part = hold[d, r if hold is r_hold else g, row : row + 16, :]
                        value = part if value is None else jnp.where(masks[at], part, value)
                        at += 1
                    value = pltpu.roll(value, (LANES - 8 * turn) & 127, 1)
                    if tile == 0:
                        out[8 * g + p, row : row + 16, 0:LANES] = value
                    else:
                        out[8 * g + p, row : row + 16, LANES:192] = value[:, 0:64]

    @pl.when(meta_ref[2] == 1)
    def _():
        for k in range(8):
            d = lax.bitwise_xor(meta_ref[0], k)
            if k >= 2:
                z_hold[d] = z_refs[k - 2][...]
            r_hold[d] = r_refs[k][...]
        for odd in range(2):

            @pl.loop(0, 8)
            def _(p):
                merge_pixels(p, odd)

    @pl.when(meta_ref[2] == 0)
    def _():
        out[...] = jnp.zeros(out.shape, BF16)


def merge_call(meta, z_parts, r_parts, dst, row0, rows):
    quad = row0 // 4
    in_specs = [pl.BlockSpec((14, BLK, LANES), lambda i, m: (i * m[2], 0, 0))] * 6
    in_specs += [pl.BlockSpec((7, BLK, LANES), lambda i, m: (quad + i * m[2], 0, 0))] * 8
    operands = [*z_parts, *r_parts]
    aliases = {}
    if dst is not None:
        in_specs.append(pl.BlockSpec(memory_space=pl.ANY))
        operands.append(dst)
        aliases = {15: 0}
    return pl.pallas_call(
        functools.partial(merge_body, aliased=dst is not None),
        grid_spec=pltpu.PrefetchScalarGridSpec(
            num_scalar_prefetch=1,
            grid=(rows // 4,),
            in_specs=in_specs,
            out_specs=pl.BlockSpec((112, BLK, 192), lambda i, m: (quad + i, 0, 0)),
            scratch_shapes=[pltpu.VMEM((8, 14, BLK, LANES), BF16), pltpu.VMEM((8, 7, BLK, LANES), BF16)],
        ),
        out_shape=jax.ShapeDtypeStruct((ROWS * COLS, BLK, 192), BF16),
        input_output_aliases=aliases,
        compiler_params=pltpu.CompilerParams(vmem_limit_bytes=VMEM_LIMIT),
        cost_estimate=pl.CostEstimate(flops=rows * 10**7, bytes_accessed=rows * COLS * BLK * 192 * 4, transcendentals=0),
    )(meta, *operands)


def patch_body(meta_ref, first, second, before, result, both_buf, part_buf, both_sem, in_sem, out_sem, *, group0):
    steps = part_buf.shape[0]

    def pixels(i):
        return pl.ds(pl.multiple_of(8 * group0 + 16 * i, 16), 16)

    def load(i):
        return pltpu.make_async_copy(before.at[pixels(i)], part_buf.at[i], in_sem.at[i])

    def store(i):
        return pltpu.make_async_copy(part_buf.at[i], result.at[pixels(i)], out_sem.at[i])

    @pl.when(meta_ref[2] == 1)
    def _():
        arrivals = [pltpu.make_async_copy(ref, both_buf.at[k], both_sem.at[k]) for k, ref in enumerate((first, second))]
        for arrival in arrivals:
            arrival.start()

        @pl.loop(0, steps)
        def _(i):
            load(i).start()

        begins = [3 * lax.bitwise_xor(meta_ref[0], k) + 1 for k in range(2)]
        lane = lax.broadcasted_iota(jnp.int32, (16, LANES), 1)
        keep = []
        for tile in range(2):
            ahead = [lane // 8 + 16 * tile - begin for begin in begins]
            mine = jnp.where(jnp.logical_or((ahead[0] & -2) == 0, (ahead[1] & -2) == 0), 1.0, 0.0)
            keep.append(mine.astype(BF16) == 1.0)
        for arrival in arrivals:
            arrival.wait()

        @pl.loop(0, steps)
        def _(i):
            load(i).wait()
            for odd in range(2):
                for p in range(8):
                    turn = 2 * p + odd
                    from_second = turned_slot(turn + begins[1]) <= 1
                    pixel = 8 * odd + p
                    for row in range(0, BLK, 16):
                        some = pl.ds(row, 16)
                        both = jnp.where(from_second, both_buf[1, 2 * i + odd, some, :], both_buf[0, 2 * i + odd, some, :])
                        both = pltpu.roll(both, (LANES - 8 * turn) & 127, 1)
                        part_buf[i, pixel, some, 0:LANES] = jnp.where(keep[0], both, part_buf[i, pixel, some, 0:LANES])
                        high = jnp.where(keep[1][:, 0:64], both[:, 0:64], part_buf[i, pixel, some, LANES:192])
                        part_buf[i, pixel, some, LANES:192] = high
            store(i).start()

        @pl.loop(0, steps)
        def _(i):
            store(i).wait()


def patch_call(meta, first, second, result, group0, groups):
    assert group0 % 2 == 0 and groups % 2 == 0
    steps = groups // 2
    return pl.pallas_call(
        functools.partial(patch_body, group0=group0),
        in_specs=[pl.BlockSpec(memory_space=pltpu.SMEM)] + [pl.BlockSpec(memory_space=pltpu.HBM)] * 3,
        out_specs=pl.BlockSpec(memory_space=pltpu.HBM),
        out_shape=jax.ShapeDtypeStruct((ROWS * COLS, BLK, 192), BF16),
        scratch_shapes=[
            pltpu.VMEM((2, groups, BLK, LANES), BF16),
            pltpu.VMEM((steps, 16, BLK, 192), BF16),
            pltpu.SemaphoreType.DMA((2,)),
            pltpu.SemaphoreType.DMA((steps,)),
            pltpu.SemaphoreType.DMA((steps,)),
        ],
        input_output_aliases={3: 0},
        compiler_params=pltpu.CompilerParams(vmem_limit_bytes=VMEM_LIMIT),
        cost_estimate=pl.CostEstimate(flops=groups * 10**6, bytes_accessed=groups * 8 * BLK * 192 * 4, transcendentals=0),
    )(meta, first, second, result)


def solution(mesh):
    def cross_pairs(k):
        return [(t, 8 + (t ^ k)) for t in range(8)]

    def late_pairs(k):
        return [(8 + t, 8 + (t ^ k)) for t in range(8)]

    def block_step(act_block, w_shard, scale_shard, shift_shard):
        pp, tp = lax.axis_index("pp"), lax.axis_index("tp")
        axes = ("pp", "tp")
        x_rows = jnp.transpose(act_block, (1, 2, 0, 3))
        raw_head = lax.ppermute(x_rows[:HEAD, :, :RAW], axes, cross_pairs(0))
        raw_tail = lax.ppermute(x_rows[HEAD:, :, :RAW], axes, cross_pairs(0))
        w_full = jnp.concatenate([lax.all_gather(w_shard[a], "tp", axis=1, tiled=True) for a in range(3)], axis=0)
        w_full = w_full.reshape(9 * CH, CH)
        affine = lax.all_gather(jnp.stack([scale_shard, shift_shard]), "tp", axis=1, tiled=True)
        scale, shift = affine[0:1], affine[1:2]
        z_meta = jnp.stack([tp, 8 * (3 * tp + 1), 1 - pp]).astype(jnp.int32)
        r_meta = jnp.stack([tp, 24 * tp, pp]).astype(jnp.int32)
        r_parts = conv_call(r_meta, (raw_head, raw_tail), w_full, scale, shift, (), 0, 7, 0, RAW, 4)
        r_recv = [r_parts[0]] + [lax.ppermute(r_parts[k], axes, late_pairs(k)) for k in range(1, 8)]
        z_recv, local_recv = [], []
        after = ()
        for c, (row0, rows) in enumerate(CROSS_CHUNKS):
            z_parts = conv_call(z_meta, (x_rows,), w_full, scale, shift, after, row0, rows // 2, RAW, LIVE, 2)
            for begin, count in LOCAL_CHUNKS[c]:
                some = slice(begin - row0 // 2 * 7, begin + count - row0 // 2 * 7)
                local_recv.append((begin, count, [lax.ppermute(z_parts[k][some], axes, cross_pairs(k)) for k in range(2)]))
            z_recv.append([lax.ppermute(z_parts[k], axes, cross_pairs(k)) for k in range(2, 8)])
            after = (z_parts[0],)
        result = None
        for (row0, rows), z_parts in zip(CROSS_CHUNKS, z_recv):
            result = merge_call(r_meta, z_parts, r_recv, result, row0, rows)
        for group0, groups, (first, second) in local_recv:
            result = patch_call(r_meta, first, second, result, group0, groups)
        return jnp.transpose(result.reshape(ROWS, COLS, BLK, 192), (3, 0, 1, 2))

    return jax.shard_map(block_step, mesh=mesh, in_specs=(P(("pp", "tp")), P(None, None, "tp", None), P("tp"), P("tp")), out_specs=P("pp", None, None, "tp"), check_vma=False)
```

time: 3030 us -> 463 us (0.15)
  the two profiles are of different devices: /device:TPU:0 before, /device:TPU:13 now
where the time goes in v1:
time: 463 us; the launch traced here: 462 us
  waiting for transfers between devices  223 us (48%)
  Pallas kernels  98.2 us (21%)
  starting transfers between devices  72 us (16%)
  blocking collectives  40.6 us (9%)
  local copies, waits for them, and re-layouts  23.2 us (5%)
    ppermute x12, waiting for transfers between devices, block_step(): lax.ppermute(z_parts[k][some], axes, cross_pairs(k))  127 us
    ppermute x12, waiting for transfers between devices, block_step(): lax.ppermute(z_parts[k], axes, cross_pairs(k))  58.5 us
    pallas_call x3, Pallas kernels, conv_call(): pl.pallas_call(functools.partial(conv_body, row0=row0, img0=img0, imgs=im...  43.1 us
    ppermute x7, starting transfers between devices, block_step(): lax.ppermute(r_parts[k], axes, late_pairs(k))  38.4 us
    ppermute x7, waiting for transfers between devices, block_step(): lax.ppermute(r_parts[k], axes, late_pairs(k))  37.4 us
    all_gather x3, blocking collectives, block_step(): lax.all_gather(w_shard[a], 'tp', axis=1, tiled=True)  31.2 us
    pallas_call x2, Pallas kernels, merge_call(): pl.pallas_call(functools.partial(merge_body, aliased=dst is not None), gr...  30.2 us
    pallas_call x6, Pallas kernels, patch_call(): pl.pallas_call(functools.partial(patch_body, group0=group0), in_specs=[pl...  24.9 us
  transfers between devices with their start and end apart: 33, of which 12 were waited for; matrix products, arithmetic and copies ran while one was open for 4% of the time, Pallas kernels for 21%

profile of v1, /device:TPU:13, one launch (start us, length us, event | category | flops | bytes accessed | tf_op | source)
XLA Modules:
  0.0 461.7 jit_solution(4793544481364088985)
XLA Ops:
  2.3 4.8 %slice.79 = bf16[26,28,8,384]{3,2,1,0:T(8,128)(2,1)} slice(bf16[28,28,24,384]{3,2,1,0:T(8,128)(2,1)} %bitcast.23), slice={[2:28], [0:28], [0:8], [0:384]} | slice | bytes 8945664 | tf_op jit(solution)/shard_map/slice | solution.py:288
  9.1 9.4 %all-gather.3 = f32[8,48,2]{1,2,0:T(2,128)S(1)} all-gather(f32[1,48,2]{1,2,0:T(2,128)S(1)} %maximum_bitcast_fusion), channel_id=1, replica_groups=mesh['pp'=2,'tp'=8] {'tp'}, dimensions={0}, use_global_device_ids=true | all-gather | bytes 3456 | tf_op jit(solution)/shard_map/all_gather | solution.py:291
  20.2 10.1 %all-gather = bf16[1,3,384,384]{3,2,1,0:T(8,128)(2,1)S(1)} all-gather(bf16[1,3,48,384]{3,2,1,0:T(8,128)(2,1)S(1)} %get-tuple-element.57), channel_id=2, replica_groups=mesh['pp'=2,'tp'=8] {'tp'}, dimensions={2}, use_global_device_ids=true | all-gather | bytes 995328 | tf_op jit(solution)/shard_map/all_gather | solution.py:289
  30.3 11.0 %all-gather.2 = bf16[1,3,384,384]{3,2,1,0:T(8,128)(2,1)S(1)} all-gather(bf16[1,3,48,384]{3,2,1,0:T(8,128)(2,1)S(1)} %get-tuple-element.58), channel_id=4, replica_groups=mesh['pp'=2,'tp'=8] {'tp'}, dimensions={2}, use_global_device_ids=true | all-gather | bytes 995328 | tf_op jit(solution)/shard_map/all_gather | solution.py:289
  41.3 10.1 %all-gather.1 = bf16[1,3,384,384]{3,2,1,0:T(8,128)(2,1)S(1)} all-gather(bf16[1,3,48,384]{3,2,1,0:T(8,128)(2,1)S(1)} %get-tuple-element.59), channel_id=3, replica_groups=mesh['pp'=2,'tp'=8] {'tp'}, dimensions={2}, use_global_device_ids=true | all-gather | bytes 995328 | tf_op jit(solution)/shard_map/all_gather | solution.py:289
  53.9 4.0 shard_map.46
  58.0 4.2 shard_map.47
  69.0 63.6 %collective-permute-done.5.second = bf16[12,48,128]{2,1,0:T(8,128)(2,1)S(1)} collective-permute-done((bf16[12,48,128]{2,1,0:T(8,128)(2,1)S(1)}, bf16[12,48,128]{2,1,0:T(8,128)(2,1)S(1)}, u32[]{:S(2)}, u32[]{:S(2)}) %collective-permute-start.5) | collective-permute-done | bytes 147488 | tf_op jit(solution)/shard_map/ppermute | solution.py:303
  143.7 21.3 %collective-permute-done.11.second = bf16[28,48,128]{2,1,0:T(8,128)(2,1)S(1)} collective-permute-done((bf16[28,48,128]{2,1,0:T(8,128)(2,1)S(1)}, bf16[28,48,128]{2,1,0:T(8,128)(2,1)S(1)}, u32[]{:S(2)}, u32[]{:S(2)}) %collective-permute-start.11) | collective-permute-done | bytes 344096 | tf_op jit(solution)/shard_map/ppermute | solution.py:303
  166.3 11.3 %collective-permute-done.9.second = bf16[28,48,128]{2,1,0:T(8,128)(2,1)S(1)} collective-permute-done((bf16[28,48,128]{2,1,0:T(8,128)(2,1)S(1)}, bf16[28,48,128]{2,1,0:T(8,128)(2,1)S(1)}, u32[]{:S(2)}, u32[]{:S(2)}) %collective-permute-start.9) | collective-permute-done | bytes 344096 | tf_op jit(solution)/shard_map/ppermute | solution.py:303
  178.9 16.8 %collective-permute-done.10.first = bf16[28,48,128]{2,1,0:T(8,128)(2,1)S(1)} collective-permute-done((bf16[28,48,128]{2,1,0:T(8,128)(2,1)S(1)}, bf16[28,48,128]{2,1,0:T(8,128)(2,1)S(1)}, u32[]{:S(2)}, u32[]{:S(2)}) %collective-permute-start.10) | collective-permute-done | bytes 344096 | tf_op jit(solution)/shard_map/ppermute | solution.py:303
  197.0 9.5 %collective-permute-done.8.first = bf16[28,48,128]{2,1,0:T(8,128)(2,1)S(1)} collective-permute-done((bf16[28,48,128]{2,1,0:T(8,128)(2,1)S(1)}, bf16[28,48,128]{2,1,0:T(8,128)(2,1)S(1)}, u32[]{:S(2)}, u32[]{:S(2)}) %collective-permute-start.8) | collective-permute-done | bytes 344096 | tf_op jit(solution)/shard_map/ppermute | solution.py:303
  212.5 49.5 %collective-permute-done.15.refs_3_ = bf16[42,48,128]{2,1,0:T(8,128)(2,1)S(1)} collective-permute-done((bf16[42,48,128]{2,1,0:T(8,128)(2,1)}, bf16[42,48,128]{2,1,0:T(8,128)(2,1)S(1)}, u32[]{:S(2)}, u32[]{:S(2)}) %collective-permute-start.15) | collective-permute-done | bytes 516128 | tf_op jit(solution)/shard_map/ppermute | solution.py:304
  270.9 34.9 %shard_map.48 = (bf16[49,48,128]{2,1,0:T(8,128)(2,1)}, bf16[49,48,128]{2,1,0:T(8,128)(2,1)}, bf16[49,48,128]{2,1,0:T(8,128)(2,1)}, bf16[49,48,128]{2,1,0:T(8,128...) custom-call(s32[3]{0:T(128)} %pad_add_fusion.meta_ref, ...), custom_call_target="tpu_custom_call" | custom-call | flops 16647192576 | bytes 9633792 | tf_op jit(solution)/shard_map/pallas_call | solution.py:97
  307.8 18.4 %collective-permute-start.21 = (bf16[49,48,128]{2,1,0:T(8,128)(2,1)}, bf16[49,48,128]{2,1,0:T(8,128)(2,1)S(1)}, u32[]{:S(2)}, u32[]{:S(2)}) collective-permute-start(bf16[49,48,128]{2,1,0:T(8,128)(2,1)} %get-tuple-element.41), channel_id=1, source_target_pairs={{8,10},{9,11},{10,8},{11,9},{12,14},{13,15},{14,12},{15,13}} | collective-permute-start | bytes 1806344 | tf_op jit(solution)/shard_map/ppermute | solution.py:296
  326.2 9.0 %collective-permute-done.30.refs_3_ = bf16[56,48,128]{2,1,0:T(8,128)(2,1)S(1)} collective-permute-done((bf16[56,48,128]{2,1,0:T(8,128)(2,1)}, bf16[56,48,128]{2,1,0:T(8,128)(2,1)S(1)}, u32[]{:S(2)}, u32[]{:S(2)}) %collective-permute-start.30) | collective-permute-done | bytes 688160 | tf_op jit(solution)/shard_map/ppermute | solution.py:304
  335.1 6.1 %collective-permute-start.22 = (bf16[49,48,128]{2,1,0:T(8,128)(2,1)}, bf16[49,48,128]{2,1,0:T(8,128)(2,1)S(1)}, u32[]{:S(2)}, u32[]{:S(2)}) collective-permute-start(bf16[49,48,128]{2,1,0:T(8,128)(2,1)} %get-tuple-element.42), channel_id=1, source_target_pairs={{8,11},{9,10},{10,9},{11,8},{12,15},{13,14},{14,13},{15,12}} | collective-permute-start | bytes 1806344 | tf_op jit(solution)/shard_map/ppermute | solution.py:296
  343.2 3.9 collective-permute-start.24
  360.2 23.7 %collective-permute-done.23.refs_10_ = bf16[49,48,128]{2,1,0:T(8,128)(2,1)S(1)} collective-permute-done((bf16[49,48,128]{2,1,0:T(8,128)(2,1)}, bf16[49,48,128]{2,1,0:T(8,128)(2,1)S(1)}, u32[]{:S(2)}, u32[]{:S(2)}) %collective-permute-start.23) | collective-permute-done | bytes 602144 | tf_op jit(solution)/shard_map/ppermute | solution.py:296
  385.2 12.2 %collective-permute-done.24.refs_11_ = bf16[49,48,128]{2,1,0:T(8,128)(2,1)S(1)} collective-permute-done((bf16[49,48,128]{2,1,0:T(8,128)(2,1)}, bf16[49,48,128]{2,1,0:T(8,128)(2,1)S(1)}, u32[]{:S(2)}, u32[]{:S(2)}) %collective-permute-start.24) | collective-permute-done | bytes 602144 | tf_op jit(solution)/shard_map/ppermute | solution.py:296
  404.4 16.7 %shard_map.49.refs_14_ = bf16[784,48,192]{2,1,0:T(8,128)(2,1)} custom-call(s32[3]{0:T(128)} %pad_add_fusion.meta_ref, bf16[56,48,128]{2,1,0:T(8,128)(2,1)} %copy-done.7, bf16[56,48,128]{2,1,0:T(8,128)(2,1)} %copy-done.8, bf16[56,48,128]{2,1,0:T(8,128)(2,1)} %copy-done.9, bf16[56,48,128]{2,1,0:T(8,128)(2,1)} %copy-done.10, bf16[56,48,128]{2,1,0:T(8,128)(2,1)} %copy-done.11, ...), custom_call_target="tpu_custom_call" | custom-call | flops 160000000 | bytes 16515072 | tf_op jit(solution)/shard_map/pallas_call | solution.py:185
  421.1 13.5 %shard_map.50.before = bf16[784,48,192]{2,1,0:T(8,128)(2,1)} custom-call(s32[3]{0:T(128)} %pad_add_fusion.meta_ref, bf16[42,48,128]{2,1,0:T(8,128)(2,1)} %collective-permute-done.12.refs_0_, bf16[42,48,128]{2,1,0:T(8,128)(2,1)} %collective-permute-done.13.refs_1_, ...), custom_call_target="tpu_custom_call", output_to_operand_aliasing={{}: (15, {})} | custom-call | flops 120000000 | bytes 12386304 | tf_op jit(solution)/shard_map/pallas_call | solution.py:185
  434.6 5.8 %shard_map.51.before = bf16[784,48,192]{2,1,0:T(8,128)(2,1)} custom-call(s32[3]{0:T(128)} %pad_add_fusion.meta_ref, bf16[28,48,128]{2,1,0:T(8,128)(2,1)} %copy-done.18, bf16[28,48,128]{2,1,0:T(8,128)(2,1)} %copy-done.16, bf16[784,48,192]{2,1,0:T(8,128)(2,1)} %shard_map.50.before), custom_call_target="tpu_custom_call", output_to_operand_aliasing={{}: (3, {})} | custom-call | flops 28000000 | bytes 8257536 | tf_op jit(solution)/shard_map/pallas_call | solution.py:258
  440.4 5.8 %shard_map.52.before = bf16[784,48,192]{2,1,0:T(8,128)(2,1)} custom-call(s32[3]{0:T(128)} %pad_add_fusion.meta_ref, bf16[28,48,128]{2,1,0:T(8,128)(2,1)} %copy-done.19, bf16[28,48,128]{2,1,0:T(8,128)(2,1)} %copy-done.17, bf16[784,48,192]{2,1,0:T(8,128)(2,1)} %shard_map.51.before), custom_call_target="tpu_custom_call", output_to_operand_aliasing={{}: (3, {})} | custom-call | flops 28000000 | bytes 8257536 | tf_op jit(solution)/shard_map/pallas_call | solution.py:258
  (131 shorter events, 85.2 us)
Async XLA Ops:
  1.0 141.3 %collective-permute-start.18 = (bf16[2,28,8,384]{3,2,1,0:T(8,128)(2,1)S(1)}, bf16[2,28,8,384]{3,2,1,0:T(8,128)(2,1)S(1)}, u32[]{:S(2)}, u32[]{:S(2)}) collective-permute-start(bf16[2,28,8,384]{3,2,1,0:T(8,128)(2,1)S(1)} %slice.78), channel_id=1, source_target_pairs={{0,8},{1,9},{2,10},{3,11},{4,12},{5,13},{6,14},{7,15}} | collective-permute-start | bytes 1032200 | tf_op jit(solution)/shard_map/ppermute | solution.py:287
  7.1 262.5 %collective-permute-start.19 = (bf16[26,28,8,384]{3,2,1,0:T(8,128)(2,1)}, bf16[26,28,8,384]{3,2,1,0:T(8,128)(2,1)}, u32[]{:S(2)}, u32[]{:S(2)}) collective-permute-start(bf16[26,28,8,384]{3,2,1,0:T(8,128)(2,1)} %slice.79), channel_id=1, source_target_pairs={{0,8},{1,9},{2,10},{3,11},{4,12},{5,13},{6,14},{7,15}} | collective-permute-start | bytes 13418504 | tf_op jit(solution)/shard_map/ppermute | solution.py:288
  63.1 69.5 %collective-permute-start.5 = (bf16[12,48,128]{2,1,0:T(8,128)(2,1)S(1)}, bf16[12,48,128]{2,1,0:T(8,128)(2,1)S(1)}, u32[]{:S(2)}, u32[]{:S(2)}) collective-permute-start(bf16[12,48,128]{2,1,0:T(8,128)(2,1)S(1)} %slice.67), channel_id=1, source_target_pairs={{0,9},{1,8},{2,11},{3,10},{4,13},{5,12},{6,15},{7,14}} | collective-permute-start | bytes 442376 | tf_op jit(solution)/shard_map/ppermute | solution.py:303
  65.3 71.2 %collective-permute-start.7 = (bf16[16,48,128]{2,1,0:T(8,128)(2,1)S(1)}, bf16[16,48,128]{2,1,0:T(8,128)(2,1)S(1)}, u32[]{:S(2)}, u32[]{:S(2)}) collective-permute-start(bf16[16,48,128]{2,1,0:T(8,128)(2,1)S(1)} %slice.69), channel_id=1, source_target_pairs={{0,9},{1,8},{2,11},{3,10},{4,13},{5,12},{6,15},{7,14}} | collective-permute-start | bytes 589832 | tf_op jit(solution)/shard_map/ppermute | solution.py:303
  67.6 72.8 %collective-permute-start.6 = (bf16[16,48,128]{2,1,0:T(8,128)(2,1)S(1)}, bf16[16,48,128]{2,1,0:T(8,128)(2,1)S(1)}, u32[]{:S(2)}, u32[]{:S(2)}) collective-permute-start(bf16[16,48,128]{2,1,0:T(8,128)(2,1)S(1)} %slice.68), channel_id=1, source_target_pairs={{0,8},{1,9},{2,10},{3,11},{4,12},{5,13},{6,14},{7,15}} | collective-permute-start | bytes 589832 | tf_op jit(solution)/shard_map/ppermute | solution.py:303
  141.1 54.6 %collective-permute-start.10 = (bf16[28,48,128]{2,1,0:T(8,128)(2,1)S(1)}, bf16[28,48,128]{2,1,0:T(8,128)(2,1)S(1)}, u32[]{:S(2)}, u32[]{:S(2)}) collective-permute-start(bf16[28,48,128]{2,1,0:T(8,128)(2,1)S(1)} %get-tuple-element.55), channel_id=1, source_target_pairs={{0,8},{1,9},{2,10},{3,11},{4,12},{5,13},{6,14},{7,15}} | collective-permute-start | bytes 1032200 | tf_op jit(solution)/shard_map/ppermute | solution.py:303
  142.4 65.4 %collective-permute-start.12 = (bf16[42,48,128]{2,1,0:T(8,128)(2,1)}, bf16[42,48,128]{2,1,0:T(8,128)(2,1)}, u32[]{:S(2)}, u32[]{:S(2)}) collective-permute-start(bf16[42,48,128]{2,1,0:T(8,128)(2,1)} %get-tuple-element.33), channel_id=1, source_target_pairs={{0,10},{1,11},{2,8},{3,9},{4,14},{5,15},{6,12},{7,13}} | collective-permute-start | bytes 1548296 | tf_op jit(solution)/shard_map/ppermute | solution.py:304
  165.0 44.1 %collective-permute-start.13 = (bf16[42,48,128]{2,1,0:T(8,128)(2,1)}, bf16[42,48,128]{2,1,0:T(8,128)(2,1)}, u32[]{:S(2)}, u32[]{:S(2)}) collective-permute-start(bf16[42,48,128]{2,1,0:T(8,128)(2,1)} %get-tuple-element.34), channel_id=1, source_target_pairs={{0,11},{1,10},{2,9},{3,8},{4,15},{5,14},{6,13},{7,12}} | collective-permute-start | bytes 1548296 | tf_op jit(solution)/shard_map/ppermute | solution.py:304
  206.5 61.8 %collective-permute-start.27 = (bf16[56,48,128]{2,1,0:T(8,128)(2,1)}, bf16[56,48,128]{2,1,0:T(8,128)(2,1)S(1)}, u32[]{:S(2)}, u32[]{:S(2)}) collective-permute-start(bf16[56,48,128]{2,1,0:T(8,128)(2,1)} %get-tuple-element.47), channel_id=1, source_target_pairs={{0,10},{1,11},{2,8},{3,9},{4,14},{5,15},{6,12},{7,13}} | collective-permute-start | bytes 2064392 | tf_op jit(solution)/shard_map/ppermute | solution.py:304
  207.8 54.2 %collective-permute-start.15 = (bf16[42,48,128]{2,1,0:T(8,128)(2,1)}, bf16[42,48,128]{2,1,0:T(8,128)(2,1)S(1)}, u32[]{:S(2)}, u32[]{:S(2)}) collective-permute-start(bf16[42,48,128]{2,1,0:T(8,128)(2,1)} %get-tuple-element.36), channel_id=1, source_target_pairs={{0,13},{1,12},{2,15},{3,14},{4,9},{5,8},{6,11},{7,10}} | collective-permute-start | bytes 1548296 | tf_op jit(solution)/shard_map/ppermute | solution.py:304
  209.1 55.0 %collective-permute-start.16 = (bf16[42,48,128]{2,1,0:T(8,128)(2,1)}, bf16[42,48,128]{2,1,0:T(8,128)(2,1)S(1)}, u32[]{:S(2)}, u32[]{:S(2)}) collective-permute-start(bf16[42,48,128]{2,1,0:T(8,128)(2,1)} %get-tuple-element.37), channel_id=1, source_target_pairs={{0,14},{1,15},{2,12},{3,13},{4,10},{5,11},{6,8},{7,9}} | collective-permute-start | bytes 1548296 | tf_op jit(solution)/shard_map/ppermute | solution.py:304
  210.6 55.6 %collective-permute-start.17 = (bf16[42,48,128]{2,1,0:T(8,128)(2,1)}, bf16[42,48,128]{2,1,0:T(8,128)(2,1)S(1)}, u32[]{:S(2)}, u32[]{:S(2)}) collective-permute-start(bf16[42,48,128]{2,1,0:T(8,128)(2,1)} %get-tuple-element.38), channel_id=1, source_target_pairs={{0,15},{1,14},{2,13},{3,12},{4,11},{5,10},{6,9},{7,8}} | collective-permute-start | bytes 1548296 | tf_op jit(solution)/shard_map/ppermute | solution.py:304
  262.8 43.0 %collective-permute-start.28 = (bf16[56,48,128]{2,1,0:T(8,128)(2,1)}, bf16[56,48,128]{2,1,0:T(8,128)(2,1)S(1)}, u32[]{:S(2)}, u32[]{:S(2)}) collective-permute-start(bf16[56,48,128]{2,1,0:T(8,128)(2,1)} %get-tuple-element.48), channel_id=1, source_target_pairs={{0,11},{1,10},{2,9},{3,8},{4,15},{5,14},{6,13},{7,12}} | collective-permute-start | bytes 2064392 | tf_op jit(solution)/shard_map/ppermute | solution.py:304
  267.0 68.1 %collective-permute-start.30 = (bf16[56,48,128]{2,1,0:T(8,128)(2,1)}, bf16[56,48,128]{2,1,0:T(8,128)(2,1)S(1)}, u32[]{:S(2)}, u32[]{:S(2)}) collective-permute-start(bf16[56,48,128]{2,1,0:T(8,128)(2,1)} %get-tuple-element.50), channel_id=1, source_target_pairs={{0,13},{1,12},{2,15},{3,14},{4,9},{5,8},{6,11},{7,10}} | collective-permute-start | bytes 2064392 | tf_op jit(solution)/shard_map/ppermute | solution.py:304
  268.3 72.9 %collective-permute-start.31 = (bf16[56,48,128]{2,1,0:T(8,128)(2,1)}, bf16[56,48,128]{2,1,0:T(8,128)(2,1)S(1)}, u32[]{:S(2)}, u32[]{:S(2)}) collective-permute-start(bf16[56,48,128]{2,1,0:T(8,128)(2,1)} %get-tuple-element.51), channel_id=1, source_target_pairs={{0,14},{1,15},{2,12},{3,13},{4,10},{5,11},{6,8},{7,9}} | collective-permute-start | bytes 2064392 | tf_op jit(solution)/shard_map/ppermute | solution.py:304
  269.6 73.6 %collective-permute-start.32 = (bf16[56,48,128]{2,1,0:T(8,128)(2,1)}, bf16[56,48,128]{2,1,0:T(8,128)(2,1)}, u32[]{:S(2)}, u32[]{:S(2)}) collective-permute-start(bf16[56,48,128]{2,1,0:T(8,128)(2,1)} %get-tuple-element.52), channel_id=1, source_target_pairs={{0,15},{1,14},{2,13},{3,12},{4,11},{5,10},{6,9},{7,8}} | collective-permute-start | bytes 2064392 | tf_op jit(solution)/shard_map/ppermute | solution.py:304
  343.2 54.2 %collective-permute-start.24 = (bf16[49,48,128]{2,1,0:T(8,128)(2,1)}, bf16[49,48,128]{2,1,0:T(8,128)(2,1)S(1)}, u32[]{:S(2)}, u32[]{:S(2)}) collective-permute-start(bf16[49,48,128]{2,1,0:T(8,128)(2,1)} %get-tuple-element.44), channel_id=1, source_target_pairs={{8,13},{9,12},{10,15},{11,14},{12,9},{13,8},{14,11},{15,10}} | collective-permute-start | bytes 1806344 | tf_op jit(solution)/shard_map/ppermute | solution.py:296
  347.2 54.5 %collective-permute-start.25 = (bf16[49,48,128]{2,1,0:T(8,128)(2,1)}, bf16[49,48,128]{2,1,0:T(8,128)(2,1)S(1)}, u32[]{:S(2)}, u32[]{:S(2)}) collective-permute-start(bf16[49,48,128]{2,1,0:T(8,128)(2,1)} %get-tuple-element.45), channel_id=1, source_target_pairs={{8,14},{9,15},{10,12},{11,13},{12,10},{13,11},{14,8},{15,9}} | collective-permute-start | bytes 1806344 | tf_op jit(solution)/shard_map/ppermute | solution.py:296
  350.3 52.7 %collective-permute-start.26 = (bf16[49,48,128]{2,1,0:T(8,128)(2,1)}, bf16[49,48,128]{2,1,0:T(8,128)(2,1)}, u32[]{:S(2)}, u32[]{:S(2)}) collective-permute-start(bf16[49,48,128]{2,1,0:T(8,128)(2,1)} %get-tuple-element.46), channel_id=1, source_target_pairs={{8,15},{9,14},{10,13},{11,12},{12,11},{13,10},{14,9},{15,8}} | collective-permute-start | bytes 1806344 | tf_op jit(solution)/shard_map/ppermute | solution.py:296
  355.9 94.1 %collective-permute-start.4 = (bf16[12,48,128]{2,1,0:T(8,128)(2,1)S(1)}, bf16[12,48,128]{2,1,0:T(8,128)(2,1)S(1)}, u32[]{:S(2)}, u32[]{:S(2)}) collective-permute-start(bf16[12,48,128]{2,1,0:T(8,128)(2,1)S(1)} %slice.66), channel_id=1, source_target_pairs={{0,8},{1,9},{2,10},{3,11},{4,12},{5,13},{6,14},{7,15}} | collective-permute-start | bytes 442376 | tf_op jit(solution)/shard_map/ppermute | solution.py:303
  383.9 70.2 %collective-permute-start.3 = (bf16[8,48,128]{2,1,0:T(8,128)(2,1)}, bf16[8,48,128]{2,1,0:T(8,128)(2,1)S(1)}, u32[]{:S(2)}, u32[]{:S(2)}) collective-permute-start(bf16[8,48,128]{2,1,0:T(8,128)(2,1)} %slice.65), channel_id=1, source_target_pairs={{0,9},{1,8},{2,11},{3,10},{4,13},{5,12},{6,15},{7,14}} | collective-permute-start | bytes 294920 | tf_op jit(solution)/shard_map/ppermute | solution.py:303
  397.4 56.8 %collective-permute-start.2 = (bf16[8,48,128]{2,1,0:T(8,128)(2,1)}, bf16[8,48,128]{2,1,0:T(8,128)(2,1)S(1)}, u32[]{:S(2)}, u32[]{:S(2)}) collective-permute-start(bf16[8,48,128]{2,1,0:T(8,128)(2,1)} %slice.64), channel_id=1, source_target_pairs={{0,8},{1,9},{2,10},{3,11},{4,12},{5,13},{6,14},{7,15}} | collective-permute-start | bytes 294920 | tf_op jit(solution)/shard_map/ppermute | solution.py:303
  401.7 56.8 %collective-permute-start.1 = (bf16[6,48,128]{2,1,0:T(8,128)(2,1)}, bf16[6,48,128]{2,1,0:T(8,128)(2,1)}, u32[]{:S(2)}, u32[]{:S(2)}) collective-permute-start(bf16[6,48,128]{2,1,0:T(8,128)(2,1)} %slice.63), channel_id=1, source_target_pairs={{0,9},{1,8},{2,11},{3,10},{4,13},{5,12},{6,15},{7,14}} | collective-permute-start | bytes 221192 | tf_op jit(solution)/shard_map/ppermute | solution.py:303
  403.0 55.5 %collective-permute-start = (bf16[6,48,128]{2,1,0:T(8,128)(2,1)}, bf16[6,48,128]{2,1,0:T(8,128)(2,1)}, u32[]{:S(2)}, u32[]{:S(2)}) collective-permute-start(bf16[6,48,128]{2,1,0:T(8,128)(2,1)} %slice.62), channel_id=1, source_target_pairs={{0,8},{1,9},{2,10},{3,11},{4,12},{5,13},{6,14},{7,15}} | collective-permute-start | bytes 221192 | tf_op jit(solution)/shard_map/ppermute | solution.py:303
  (36 other events, 859.8 us)

commit v2 on v1

--- a/solution.py
+++ b/solution.py
@@ -19,9 +19,11 @@
 LIVE = IMGS - RAW
 LANES = 128
 VMEM_LIMIT = 60 * 1024 * 1024
+PATCH_VMEM_LIMIT = 16 * 1024 * 1024
 HEAD = 2
+FETCHED = 2
 CROSS_CHUNKS = ((0, 16), (16, 12))
-LOCAL_CHUNKS = (((0, 28), (28, 28)), ((56, 16), (72, 12), (84, 8), (92, 6)))
+LOCAL_CHUNKS = (((0, 28), (28, 28)), ((56, 16), (72, 14), (86, 6), (92, 6)))
 
 
 def conv_body(meta_ref, *refs, **sizes):
@@ -198,41 +200,58 @@
     )(meta, *operands)
 
 
-def patch_body(meta_ref, first, second, before, result, both_buf, part_buf, both_sem, in_sem, out_sem, *, group0):
-    steps = part_buf.shape[0]
-
-    def pixels(i):
-        return pl.ds(pl.multiple_of(8 * group0 + 16 * i, 16), 16)
+def patch_body(meta_ref, first, second, *refs, group0, steps, ahead, given):
+    refs = list(refs)
+    part_buf = refs.pop(0) if given else None
+    before, result = refs.pop(0), refs.pop(0)
+    fetched, fetch_sem = (refs.pop(0), refs.pop(-1)) if ahead else (None, None)
+    out_buf, out_sem = refs[:2]
+    if not given:
+        both_buf, both_sem, in_sem = refs[2:]
+        part_buf = out_buf
+
+    def pixels(start, i):
+        return pl.ds(pl.multiple_of(8 * start + 16 * i, 16), 16)
 
     def load(i):
-        return pltpu.make_async_copy(before.at[pixels(i)], part_buf.at[i], in_sem.at[i])
+        return pltpu.make_async_copy(before.at[pixels(group0, i)], part_buf.at[i], in_sem.at[i])
 
     def store(i):
-        return pltpu.make_async_copy(part_buf.at[i], result.at[pixels(i)], out_sem.at[i])
+        return pltpu.make_async_copy(out_buf.at[i], result.at[pixels(group0, i)], out_sem.at[i])
+
+    def fetch(i):
+        return pltpu.make_async_copy(before.at[pixels(ahead[0], i)], fetched.at[i], fetch_sem.at[i])
 
     @pl.when(meta_ref[2] == 1)
     def _():
-        arrivals = [pltpu.make_async_copy(ref, both_buf.at[k], both_sem.at[k]) for k, ref in enumerate((first, second))]
-        for arrival in arrivals:
-            arrival.start()
-
-        @pl.loop(0, steps)
-        def _(i):
-            load(i).start()
+        if not given:
+            arrivals = [pltpu.make_async_copy(ref, both_buf.at[k], both_sem.at[k]) for k, ref in enumerate((first, second))]
+            for arrival in arrivals:
+                arrival.start()
+
+            @pl.loop(0, steps)
+            def _(i):
+                load(i).start()
+
+        if ahead:
+            for i in range(ahead[1]):
+                fetch(i).start()
 
         begins = [3 * lax.bitwise_xor(meta_ref[0], k) + 1 for k in range(2)]
         lane = lax.broadcasted_iota(jnp.int32, (16, LANES), 1)
         keep = []
         for tile in range(2):
-            ahead = [lane // 8 + 16 * tile - begin for begin in begins]
-            mine = jnp.where(jnp.logical_or((ahead[0] & -2) == 0, (ahead[1] & -2) == 0), 1.0, 0.0)
+            past = [lane // 8 + 16 * tile - begin for begin in begins]
+            mine = jnp.where(jnp.logical_or((past[0] & -2) == 0, (past[1] & -2) == 0), 1.0, 0.0)
             keep.append(mine.astype(BF16) == 1.0)
-        for arrival in arrivals:
-            arrival.wait()
+        if not given:
+            for arrival in arrivals:
+                arrival.wait()
 
         @pl.loop(0, steps)
         def _(i):
-            load(i).wait()
+            if not given:
+                load(i).wait()
             for odd in range(2):
                 for p in range(8):
                     turn = 2 * p + odd
@@ -240,37 +259,53 @@
                     pixel = 8 * odd + p
                     for row in range(0, BLK, 16):
                         some = pl.ds(row, 16)
-                        both = jnp.where(from_second, both_buf[1, 2 * i + odd, some, :], both_buf[0, 2 * i + odd, some, :])
+                        if given:
+                            pair = [ref[2 * i + odd, some, :] for ref in (first, second)]
+                        else:
+                            pair = [both_buf[k, 2 * i + odd, some, :] for k in range(2)]
+                        both = jnp.where(from_second, pair[1], pair[0])
                         both = pltpu.roll(both, (LANES - 8 * turn) & 127, 1)
-                        part_buf[i, pixel, some, 0:LANES] = jnp.where(keep[0], both, part_buf[i, pixel, some, 0:LANES])
+                        out_buf[i, pixel, some, 0:LANES] = jnp.where(keep[0], both, part_buf[i, pixel, some, 0:LANES])
                         high = jnp.where(keep[1][:, 0:64], both[:, 0:64], part_buf[i, pixel, some, LANES:192])
-                        part_buf[i, pixel, some, LANES:192] = high
+                        out_buf[i, pixel, some, LANES:192] = high
             store(i).start()
 
         @pl.loop(0, steps)
         def _(i):
             store(i).wait()
 
-
-def patch_call(meta, first, second, result, group0, groups):
+        if ahead:
+            for i in range(ahead[1]):
+                fetch(i).wait()
+
+
+def patch_call(meta, first, second, result, group0, groups, ahead, part):
     assert group0 % 2 == 0 and groups % 2 == 0
     steps = groups // 2
-    return pl.pallas_call(
-        functools.partial(patch_body, group0=group0),
-        in_specs=[pl.BlockSpec(memory_space=pltpu.SMEM)] + [pl.BlockSpec(memory_space=pltpu.HBM)] * 3,
-        out_specs=pl.BlockSpec(memory_space=pltpu.HBM),
-        out_shape=jax.ShapeDtypeStruct((ROWS * COLS, BLK, 192), BF16),
-        scratch_shapes=[
-            pltpu.VMEM((2, groups, BLK, LANES), BF16),
-            pltpu.VMEM((steps, 16, BLK, 192), BF16),
-            pltpu.SemaphoreType.DMA((2,)),
-            pltpu.SemaphoreType.DMA((steps,)),
-            pltpu.SemaphoreType.DMA((steps,)),
-        ],
-        input_output_aliases={3: 0},
-        compiler_params=pltpu.CompilerParams(vmem_limit_bytes=VMEM_LIMIT),
+    given = part is not None
+    hbm, vmem = pl.BlockSpec(memory_space=pltpu.HBM), pl.BlockSpec(memory_space=pltpu.VMEM)
+    in_specs = [pl.BlockSpec(memory_space=pltpu.SMEM)] + ([vmem] * 3 if given else [hbm] * 2) + [hbm]
+    operands = [meta, first, second] + ([part] if given else []) + [result]
+    out_specs, out_shape = [hbm], [jax.ShapeDtypeStruct((ROWS * COLS, BLK, 192), BF16)]
+    scratch = [pltpu.VMEM((steps, 16, BLK, 192), BF16), pltpu.SemaphoreType.DMA((steps,))]
+    if not given:
+        scratch += [pltpu.VMEM((2, groups, BLK, LANES), BF16), pltpu.SemaphoreType.DMA((2,)), pltpu.SemaphoreType.DMA((steps,))]
+    if ahead:
+        ahead = (ahead[0], ahead[1] // 2)
+        out_specs.append(vmem)
+        out_shape.append(pltpu.VMEM((ahead[1], 16, BLK, 192), BF16))
+        scratch.append(pltpu.SemaphoreType.DMA((ahead[1],)))
+    out = pl.pallas_call(
+        functools.partial(patch_body, group0=group0, steps=steps, ahead=ahead, given=given),
+        in_specs=in_specs,
+        out_specs=out_specs,
+        out_shape=out_shape,
+        scratch_shapes=scratch,
+        input_output_aliases={len(operands) - 1: 0},
+        compiler_params=pltpu.CompilerParams(vmem_limit_bytes=PATCH_VMEM_LIMIT),
         cost_estimate=pl.CostEstimate(flops=groups * 10**6, bytes_accessed=groups * 8 * BLK * 192 * 4, transcendentals=0),
-    )(meta, first, second, result)
+    )(*operands)
+    return out if ahead else out[0]
 
 
 def solution(mesh):
@@ -282,32 +317,48 @@
 
     def block_step(act_block, w_shard, scale_shard, shift_shard):
         pp, tp = lax.axis_index("pp"), lax.axis_index("tp")
-        axes = ("pp", "tp")
+
+        def send(value, pairs):
+            return lax.ppermute(value, ("pp", "tp"), pairs)
+
         x_rows = jnp.transpose(act_block, (1, 2, 0, 3))
-        raw_head = lax.ppermute(x_rows[:HEAD, :, :RAW], axes, cross_pairs(0))
-        raw_tail = lax.ppermute(x_rows[HEAD:, :, :RAW], axes, cross_pairs(0))
+        raw_head = send(x_rows[:HEAD, :, :RAW], cross_pairs(0))
+        raw_tail = send(x_rows[HEAD:, :, :RAW], cross_pairs(0))
         w_full = jnp.concatenate([lax.all_gather(w_shard[a], "tp", axis=1, tiled=True) for a in range(3)], axis=0)
         w_full = w_full.reshape(9 * CH, CH)
         affine = lax.all_gather(jnp.stack([scale_shard, shift_shard]), "tp", axis=1, tiled=True)
         scale, shift = affine[0:1], affine[1:2]
         z_meta = jnp.stack([tp, 8 * (3 * tp + 1), 1 - pp]).astype(jnp.int32)
         r_meta = jnp.stack([tp, 24 * tp, pp]).astype(jnp.int32)
+
+        def live(c, after):
+            row0, rows = CROSS_CHUNKS[c]
+            return conv_call(z_meta, (x_rows,), w_full, scale, shift, after, row0, rows // 2, RAW, LIVE, 2)
+
+        def send_local(c, z_parts):
+            base = CROSS_CHUNKS[c][0] // 2 * 7
+            return [(g, n, [send(z_parts[k][g - base : g - base + n], cross_pairs(k)) for k in range(2)]) for g, n in LOCAL_CHUNKS[c]]
+
+        def send_cross(z_parts):
+            return [send(z_parts[k], cross_pairs(k)) for k in range(2, 8)]
+
+        z_parts = live(0, ())
+        local_recv = send_local(0, z_parts)
+        z_recv = [send_cross(z_parts)]
         r_parts = conv_call(r_meta, (raw_head, raw_tail), w_full, scale, shift, (), 0, 7, 0, RAW, 4)
-        r_recv = [r_parts[0]] + [lax.ppermute(r_parts[k], axes, late_pairs(k)) for k in range(1, 8)]
-        z_recv, local_recv = [], []
-        after = ()
-        for c, (row0, rows) in enumerate(CROSS_CHUNKS):
-            z_parts = conv_call(z_meta, (x_rows,), w_full, scale, shift, after, row0, rows // 2, RAW, LIVE, 2)
-            for begin, count in LOCAL_CHUNKS[c]:
-                some = slice(begin - row0 // 2 * 7, begin + count - row0 // 2 * 7)
-                local_recv.append((begin, count, [lax.ppermute(z_parts[k][some], axes, cross_pairs(k)) for k in range(2)]))
-            z_recv.append([lax.ppermute(z_parts[k], axes, cross_pairs(k)) for k in range(2, 8)])
-            after = (z_parts[0],)
+        r_recv = [r_parts[0]] + [send(r_parts[k], late_pairs(k)) for k in range(1, 8)]
+        z_parts = live(1, (z_parts[0],))
+        z_recv.append(send_cross(z_parts))
+        local_recv += send_local(1, z_parts)
         result = None
         for (row0, rows), z_parts in zip(CROSS_CHUNKS, z_recv):
             result = merge_call(r_meta, z_parts, r_recv, result, row0, rows)
-        for group0, groups, (first, second) in local_recv:
-            result = patch_call(r_meta, first, second, result, group0, groups)
+        parts = {}
+        for n, (group0, groups, (first, second)) in enumerate(local_recv):
+            ahead = local_recv[n + 2][:2] if n + 2 >= len(local_recv) - FETCHED and n + 2 < len(local_recv) else None
+            result = patch_call(r_meta, first, second, result, group0, groups, ahead, parts.get(n))
+            if ahead:
+                result, parts[n + 2] = result
         return jnp.transpose(result.reshape(ROWS, COLS, BLK, 192), (3, 0, 1, 2))
 
     return jax.shard_map(block_step, mesh=mesh, in_specs=(P(("pp", "tp")), P(None, None, "tp", None), P("tp"), P("tp")), out_specs=P("pp", None, None, "tp"), check_vma=False)

time: 463 us -> 455 us (0.983)
  local copies, waits for them, and re-layouts: 23.2 us -> 11.3 us
  waiting for transfers between devices: 223 us -> 228 us
    slice x12 -> x10, local copies, waits for them, and re-layouts: 15.8 us -> 9.7 us  [the longest x1 4.82 us: block_step(): raw_tail = send(x_rows[HEAD:, :, :RAW], cross_pairs(0))]
    ppermute x33, waiting for transfers between devices: 223 us -> 228 us  [send(): return lax.ppermute(value, ('pp', 'tp'), pairs)]
    unnamed x55 -> x37, local copies, waits for them, and re-layouts: 5.79 us -> 0.94 us
  transfers between devices with their start and end apart: 33 -> 33, of which waited for: 12 -> 12; matrix products, arithmetic and copies ran while one was open for 4% -> 3% of each run, Pallas kernels for 21% -> 21%
where the time goes in v2:
time: 455 us; the launch traced here: 454 us
  waiting for transfers between devices  228 us (50%)
  Pallas kernels  96.1 us (21%)
  starting transfers between devices  73.8 us (16%)
  blocking collectives  40.6 us (9%)
  local copies, waits for them, and re-layouts  11.3 us (2%)
    ppermute x33, waiting for transfers between devices, send(): return lax.ppermute(value, ('pp', 'tp'), pairs)  228 us
    ppermute x33, starting transfers between devices, send(): return lax.ppermute(value, ('pp', 'tp'), pairs)  73.8 us
    pallas_call x3, Pallas kernels, conv_call(): pl.pallas_call(functools.partial(conv_body, row0=row0, img0=img0, imgs=im...  43.1 us
    all_gather x3, blocking collectives, block_step(): lax.all_gather(w_shard[a], 'tp', axis=1, tiled=True)  31.2 us
    pallas_call x2, Pallas kernels, merge_call(): pl.pallas_call(functools.partial(merge_body, aliased=dst is not None), gr...  30.2 us
    pallas_call x6, Pallas kernels, patch_call(): pl.pallas_call(functools.partial(patch_body, group0=group0, steps=steps,...  22.8 us
    all_gather x1, blocking collectives, block_step(): lax.all_gather(jnp.stack([scale_shard, shift_shard]), 'tp', axis=1, tiled...  9.42 us
  transfers between devices with their start and end apart: 33, of which 12 were waited for; matrix products, arithmetic and copies ran while one was open for 3% of the time, Pallas kernels for 21%

profile of v2, /device:TPU:13, one launch (start us, length us, event | category | flops | bytes accessed | tf_op | source)
XLA Modules:
  0.0 453.8 jit_solution(3976561440834546900)
XLA Ops:
  2.5 4.8 %slice.79 = bf16[26,28,8,384]{3,2,1,0:T(8,128)(2,1)} slice(bf16[28,28,24,384]{3,2,1,0:T(8,128)(2,1)} %bitcast.23), slice={[2:28], [0:28], [0:8], [0:384]} | slice | bytes 8945664 | tf_op jit(solution)/shard_map/slice | solution.py:326
  8.6 9.4 %all-gather.3 = f32[8,48,2]{1,2,0:T(2,128)S(1)} all-gather(f32[1,48,2]{1,2,0:T(2,128)S(1)} %maximum_bitcast_fusion), channel_id=1, replica_groups=mesh['pp'=2,'tp'=8] {'tp'}, dimensions={0}, use_global_device_ids=true | all-gather | bytes 3456 | tf_op jit(solution)/shard_map/all_gather | solution.py:329
  18.8 10.1 %all-gather = bf16[1,3,384,384]{3,2,1,0:T(8,128)(2,1)S(1)} all-gather(bf16[1,3,48,384]{3,2,1,0:T(8,128)(2,1)S(1)} %get-tuple-element.69), channel_id=2, replica_groups=mesh['pp'=2,'tp'=8] {'tp'}, dimensions={2}, use_global_device_ids=true | all-gather | bytes 995328 | tf_op jit(solution)/shard_map/all_gather | solution.py:327
  28.9 11.0 %all-gather.2 = bf16[1,3,384,384]{3,2,1,0:T(8,128)(2,1)S(1)} all-gather(bf16[1,3,48,384]{3,2,1,0:T(8,128)(2,1)S(1)} %get-tuple-element.70), channel_id=4, replica_groups=mesh['pp'=2,'tp'=8] {'tp'}, dimensions={2}, use_global_device_ids=true | all-gather | bytes 995328 | tf_op jit(solution)/shard_map/all_gather | solution.py:327
  39.9 10.1 %all-gather.1 = bf16[1,3,384,384]{3,2,1,0:T(8,128)(2,1)S(1)} all-gather(bf16[1,3,48,384]{3,2,1,0:T(8,128)(2,1)S(1)} %get-tuple-element.71), channel_id=3, replica_groups=mesh['pp'=2,'tp'=8] {'tp'}, dimensions={2}, use_global_device_ids=true | all-gather | bytes 995328 | tf_op jit(solution)/shard_map/all_gather | solution.py:327
  52.4 4.1 shard_map.46
  56.5 4.2 shard_map.47
  67.5 64.2 %collective-permute-done.3.second = bf16[14,48,128]{2,1,0:T(8,128)(2,1)S(1)} collective-permute-done((bf16[14,48,128]{2,1,0:T(8,128)(2,1)S(1)}, bf16[14,48,128]{2,1,0:T(8,128)(2,1)S(1)}, u32[]{:S(2)}, u32[]{:S(2)}) %collective-permute-start.3) | collective-permute-done | bytes 172064 | tf_op jit(solution)/shard_map/ppermute | solution.py:322
  142.0 16.5 %collective-permute-done.9.second = bf16[28,48,128]{2,1,0:T(8,128)(2,1)S(1)} collective-permute-done((bf16[28,48,128]{2,1,0:T(8,128)(2,1)S(1)}, bf16[28,48,128]{2,1,0:T(8,128)(2,1)S(1)}, u32[]{:S(2)}, u32[]{:S(2)}) %collective-permute-start.9) | collective-permute-done | bytes 344096 | tf_op jit(solution)/shard_map/ppermute | solution.py:322
  159.8 16.8 %collective-permute-done.7.second = bf16[28,48,128]{2,1,0:T(8,128)(2,1)S(1)} collective-permute-done((bf16[28,48,128]{2,1,0:T(8,128)(2,1)S(1)}, bf16[28,48,128]{2,1,0:T(8,128)(2,1)S(1)}, u32[]{:S(2)}, u32[]{:S(2)}) %collective-permute-start.7) | collective-permute-done | bytes 344096 | tf_op jit(solution)/shard_map/ppermute | solution.py:322
  178.0 16.8 %collective-permute-done.8.first = bf16[28,48,128]{2,1,0:T(8,128)(2,1)S(1)} collective-permute-done((bf16[28,48,128]{2,1,0:T(8,128)(2,1)S(1)}, bf16[28,48,128]{2,1,0:T(8,128)(2,1)S(1)}, u32[]{:S(2)}, u32[]{:S(2)}) %collective-permute-start.8) | collective-permute-done | bytes 344096 | tf_op jit(solution)/shard_map/ppermute | solution.py:322
  196.0 9.5 %collective-permute-done.6.first = bf16[28,48,128]{2,1,0:T(8,128)(2,1)S(1)} collective-permute-done((bf16[28,48,128]{2,1,0:T(8,128)(2,1)S(1)}, bf16[28,48,128]{2,1,0:T(8,128)(2,1)S(1)}, u32[]{:S(2)}, u32[]{:S(2)}) %collective-permute-start.6) | collective-permute-done | bytes 344096 | tf_op jit(solution)/shard_map/ppermute | solution.py:322
  211.6 49.5 %collective-permute-done.13.refs_3_ = bf16[42,48,128]{2,1,0:T(8,128)(2,1)S(1)} collective-permute-done((bf16[42,48,128]{2,1,0:T(8,128)(2,1)}, bf16[42,48,128]{2,1,0:T(8,128)(2,1)S(1)}, u32[]{:S(2)}, u32[]{:S(2)}) %collective-permute-start.13) | collective-permute-done | bytes 516128 | tf_op jit(solution)/shard_map/ppermute | solution.py:322
  268.5 34.9 %shard_map.48 = (bf16[49,48,128]{2,1,0:T(8,128)(2,1)}, bf16[49,48,128]{2,1,0:T(8,128)(2,1)}, bf16[49,48,128]{2,1,0:T(8,128)(2,1)}, bf16[49,48,128]{2,1,0:T(8,128...) custom-call(s32[3]{0:T(128)} %pad_add_fusion.meta_ref, ...), custom_call_target="tpu_custom_call" | custom-call | flops 16647192576 | bytes 9633792 | tf_op jit(solution)/shard_map/pallas_call | solution.py:99
  305.4 19.9 %collective-permute-start.19 = (bf16[49,48,128]{2,1,0:T(8,128)(2,1)}, bf16[49,48,128]{2,1,0:T(8,128)(2,1)S(1)}, u32[]{:S(2)}, u32[]{:S(2)}) collective-permute-start(bf16[49,48,128]{2,1,0:T(8,128)(2,1)} %get-tuple-element.45), channel_id=1, source_target_pairs={{8,10},{9,11},{10,8},{11,9},{12,14},{13,15},{14,12},{15,13}} | collective-permute-start | bytes 1806344 | tf_op jit(solution)/shard_map/ppermute | solution.py:322
  325.3 9.0 %collective-permute-done.28.refs_3_ = bf16[56,48,128]{2,1,0:T(8,128)(2,1)} collective-permute-done((bf16[56,48,128]{2,1,0:T(8,128)(2,1)}, bf16[56,48,128]{2,1,0:T(8,128)(2,1)}, u32[]{:S(2)}, u32[]{:S(2)}) %collective-permute-start.28) | collective-permute-done | bytes 688160 | tf_op jit(solution)/shard_map/ppermute | solution.py:322
  334.3 6.1 %collective-permute-start.20 = (bf16[49,48,128]{2,1,0:T(8,128)(2,1)}, bf16[49,48,128]{2,1,0:T(8,128)(2,1)S(1)}, u32[]{:S(2)}, u32[]{:S(2)}) collective-permute-start(bf16[49,48,128]{2,1,0:T(8,128)(2,1)} %get-tuple-element.46), channel_id=1, source_target_pairs={{8,11},{9,10},{10,9},{11,8},{12,15},{13,14},{14,13},{15,12}} | collective-permute-start | bytes 1806344 | tf_op jit(solution)/shard_map/ppermute | solution.py:322
  357.2 25.8 %collective-permute-done.21.refs_10_ = bf16[49,48,128]{2,1,0:T(8,128)(2,1)S(1)} collective-permute-done((bf16[49,48,128]{2,1,0:T(8,128)(2,1)}, bf16[49,48,128]{2,1,0:T(8,128)(2,1)S(1)}, u32[]{:S(2)}, u32[]{:S(2)}) %collective-permute-start.21) | collective-permute-done | bytes 602144 | tf_op jit(solution)/shard_map/ppermute | solution.py:322
  384.3 12.2 %collective-permute-done.22.refs_11_ = bf16[49,48,128]{2,1,0:T(8,128)(2,1)S(1)} collective-permute-done((bf16[49,48,128]{2,1,0:T(8,128)(2,1)}, bf16[49,48,128]{2,1,0:T(8,128)(2,1)S(1)}, u32[]{:S(2)}, u32[]{:S(2)}) %collective-permute-start.22) | collective-permute-done | bytes 602144 | tf_op jit(solution)/shard_map/ppermute | solution.py:322
  400.5 16.7 %shard_map.49.refs_14_ = bf16[784,48,192]{2,1,0:T(8,128)(2,1)} custom-call(s32[3]{0:T(128)} %pad_add_fusion.meta_ref, bf16[56,48,128]{2,1,0:T(8,128)(2,1)} %copy-done.9, bf16[56,48,128]{2,1,0:T(8,128)(2,1)} %copy-done.10, bf16[56,48,128]{2,1,0:T(8,128)(2,1)} %collective-permute-done.27.refs_2_, bf16[56,48,128]{2,1,0:T(8,128)(2,1)} %collective-permute-done.28.refs_3_, ...), custom_call_target="tpu_custom_call" | custom-call | flops 160000000 | bytes 16515072 | tf_op jit(solution)/shard_map/pallas_call | solution.py:187
  417.2 13.5 %shard_map.50.refs_0_ = bf16[784,48,192]{2,1,0:T(8,128)(2,1)} custom-call(s32[3]{0:T(128)} %pad_add_fusion.meta_ref, bf16[42,48,128]{2,1,0:T(8,128)(2,1)} %collective-permute-done.10.refs_0_, bf16[42,48,128]{2,1,0:T(8,128)(2,1)} %collective-permute-done.11.refs_1_, ...), custom_call_target="tpu_custom_call", output_to_operand_aliasing={{}: (15, {})} | custom-call | flops 120000000 | bytes 12386304 | tf_op jit(solution)/shard_map/pallas_call | solution.py:187
  430.8 5.8 %shard_map.51.refs_0_ = bf16[784,48,192]{2,1,0:T(8,128)(2,1)} custom-call(s32[3]{0:T(128)S(1)} %copy-done, bf16[28,48,128]{2,1,0:T(8,128)(2,1)S(1)} %collective-permute-done.8.first, bf16[28,48,128]{2,1,0:T(8,128)(2,1)S(1)} %collective-permute-done.9.second, bf16[784,48,192]{2,1,0:T(8,128)(2,1)} %shard_map.50.refs_0_), custom_call_target="tpu_custom_call", output_to_operand_aliasing={{}: (3, {})} | custom-call | flops 28000000 | bytes 8257536 | tf_op jit(solution)/shard_map/pallas_call | solution.py:298
  436.5 5.8 %shard_map.52.refs_0_ = bf16[784,48,192]{2,1,0:T(8,128)(2,1)} custom-call(s32[3]{0:T(128)S(1)} %copy-done, bf16[28,48,128]{2,1,0:T(8,128)(2,1)S(1)} %collective-permute-done.6.first, bf16[28,48,128]{2,1,0:T(8,128)(2,1)S(1)} %collective-permute-done.7.second, bf16[784,48,192]{2,1,0:T(8,128)(2,1)} %shard_map.51.refs_0_), custom_call_target="tpu_custom_call", output_to_operand_aliasing={{}: (3, {})} | custom-call | flops 28000000 | bytes 8257536 | tf_op jit(solution)/shard_map/pallas_call | solution.py:298
  442.3 4.0 shard_map.53
  (111 shorter events, 72.3 us)
Async XLA Ops:
  1.1 139.7 %collective-permute-start.16 = (bf16[2,28,8,384]{3,2,1,0:T(8,128)(2,1)S(1)}, bf16[2,28,8,384]{3,2,1,0:T(8,128)(2,1)S(1)}, u32[]{:S(2)}, u32[]{:S(2)}) collective-permute-start(bf16[2,28,8,384]{3,2,1,0:T(8,128)(2,1)S(1)} %slice.78), channel_id=1, source_target_pairs={{0,8},{1,9},{2,10},{3,11},{4,12},{5,13},{6,14},{7,15}} | collective-permute-start | bytes 1032200 | tf_op jit(solution)/shard_map/ppermute | solution.py:322
  7.3 259.8 %collective-permute-start.17 = (bf16[26,28,8,384]{3,2,1,0:T(8,128)(2,1)}, bf16[26,28,8,384]{3,2,1,0:T(8,128)(2,1)}, u32[]{:S(2)}, u32[]{:S(2)}) collective-permute-start(bf16[26,28,8,384]{3,2,1,0:T(8,128)(2,1)} %slice.79), channel_id=1, source_target_pairs={{0,8},{1,9},{2,10},{3,11},{4,12},{5,13},{6,14},{7,15}} | collective-permute-start | bytes 13418504 | tf_op jit(solution)/shard_map/ppermute | solution.py:322
  61.6 70.1 %collective-permute-start.3 = (bf16[14,48,128]{2,1,0:T(8,128)(2,1)S(1)}, bf16[14,48,128]{2,1,0:T(8,128)(2,1)S(1)}, u32[]{:S(2)}, u32[]{:S(2)}) collective-permute-start(bf16[14,48,128]{2,1,0:T(8,128)(2,1)S(1)} %slice.65), channel_id=1, source_target_pairs={{0,9},{1,8},{2,11},{3,10},{4,13},{5,12},{6,15},{7,14}} | collective-permute-start | bytes 516104 | tf_op jit(solution)/shard_map/ppermute | solution.py:322
  63.8 71.7 %collective-permute-start.5 = (bf16[16,48,128]{2,1,0:T(8,128)(2,1)S(1)}, bf16[16,48,128]{2,1,0:T(8,128)(2,1)S(1)}, u32[]{:S(2)}, u32[]{:S(2)}) collective-permute-start(bf16[16,48,128]{2,1,0:T(8,128)(2,1)S(1)} %slice.67), channel_id=1, source_target_pairs={{0,9},{1,8},{2,11},{3,10},{4,13},{5,12},{6,15},{7,14}} | collective-permute-start | bytes 589832 | tf_op jit(solution)/shard_map/ppermute | solution.py:322
  66.1 73.3 %collective-permute-start.4 = (bf16[16,48,128]{2,1,0:T(8,128)(2,1)S(1)}, bf16[16,48,128]{2,1,0:T(8,128)(2,1)S(1)}, u32[]{:S(2)}, u32[]{:S(2)}) collective-permute-start(bf16[16,48,128]{2,1,0:T(8,128)(2,1)S(1)} %slice.66), channel_id=1, source_target_pairs={{0,8},{1,9},{2,10},{3,11},{4,12},{5,13},{6,14},{7,15}} | collective-permute-start | bytes 589832 | tf_op jit(solution)/shard_map/ppermute | solution.py:322
  139.4 55.3 %collective-permute-start.8 = (bf16[28,48,128]{2,1,0:T(8,128)(2,1)S(1)}, bf16[28,48,128]{2,1,0:T(8,128)(2,1)S(1)}, u32[]{:S(2)}, u32[]{:S(2)}) collective-permute-start(bf16[28,48,128]{2,1,0:T(8,128)(2,1)S(1)} %get-tuple-element.63), channel_id=1, source_target_pairs={{0,8},{1,9},{2,10},{3,11},{4,12},{5,13},{6,14},{7,15}} | collective-permute-start | bytes 1032200 | tf_op jit(solution)/shard_map/ppermute | solution.py:322
  140.7 66.1 %collective-permute-start.10 = (bf16[42,48,128]{2,1,0:T(8,128)(2,1)}, bf16[42,48,128]{2,1,0:T(8,128)(2,1)}, u32[]{:S(2)}, u32[]{:S(2)}) collective-permute-start(bf16[42,48,128]{2,1,0:T(8,128)(2,1)} %get-tuple-element.37), channel_id=1, source_target_pairs={{0,10},{1,11},{2,8},{3,9},{4,14},{5,15},{6,12},{7,13}} | collective-permute-start | bytes 1548296 | tf_op jit(solution)/shard_map/ppermute | solution.py:322
  158.5 49.6 %collective-permute-start.11 = (bf16[42,48,128]{2,1,0:T(8,128)(2,1)}, bf16[42,48,128]{2,1,0:T(8,128)(2,1)}, u32[]{:S(2)}, u32[]{:S(2)}) collective-permute-start(bf16[42,48,128]{2,1,0:T(8,128)(2,1)} %get-tuple-element.38), channel_id=1, source_target_pairs={{0,11},{1,10},{2,9},{3,8},{4,15},{5,14},{6,13},{7,12}} | collective-permute-start | bytes 1548296 | tf_op jit(solution)/shard_map/ppermute | solution.py:322
  205.5 60.2 %collective-permute-start.25 = (bf16[56,48,128]{2,1,0:T(8,128)(2,1)}, bf16[56,48,128]{2,1,0:T(8,128)(2,1)S(1)}, u32[]{:S(2)}, u32[]{:S(2)}) collective-permute-start(bf16[56,48,128]{2,1,0:T(8,128)(2,1)} %get-tuple-element.51), channel_id=1, source_target_pairs={{0,10},{1,11},{2,8},{3,9},{4,14},{5,15},{6,12},{7,13}} | collective-permute-start | bytes 2064392 | tf_op jit(solution)/shard_map/ppermute | solution.py:322
  206.8 54.2 %collective-permute-start.13 = (bf16[42,48,128]{2,1,0:T(8,128)(2,1)}, bf16[42,48,128]{2,1,0:T(8,128)(2,1)S(1)}, u32[]{:S(2)}, u32[]{:S(2)}) collective-permute-start(bf16[42,48,128]{2,1,0:T(8,128)(2,1)} %get-tuple-element.40), channel_id=1, source_target_pairs={{0,13},{1,12},{2,15},{3,14},{4,9},{5,8},{6,11},{7,10}} | collective-permute-start | bytes 1548296 | tf_op jit(solution)/shard_map/ppermute | solution.py:322
  208.1 55.0 %collective-permute-start.14 = (bf16[42,48,128]{2,1,0:T(8,128)(2,1)}, bf16[42,48,128]{2,1,0:T(8,128)(2,1)}, u32[]{:S(2)}, u32[]{:S(2)}) collective-permute-start(bf16[42,48,128]{2,1,0:T(8,128)(2,1)} %get-tuple-element.41), channel_id=1, source_target_pairs={{0,14},{1,15},{2,12},{3,13},{4,10},{5,11},{6,8},{7,9}} | collective-permute-start | bytes 1548296 | tf_op jit(solution)/shard_map/ppermute | solution.py:322
  209.6 54.8 %collective-permute-start.15 = (bf16[42,48,128]{2,1,0:T(8,128)(2,1)}, bf16[42,48,128]{2,1,0:T(8,128)(2,1)}, u32[]{:S(2)}, u32[]{:S(2)}) collective-permute-start(bf16[42,48,128]{2,1,0:T(8,128)(2,1)} %get-tuple-element.42), channel_id=1, source_target_pairs={{0,15},{1,14},{2,13},{3,12},{4,11},{5,10},{6,9},{7,8}} | collective-permute-start | bytes 1548296 | tf_op jit(solution)/shard_map/ppermute | solution.py:322
  264.4 69.8 %collective-permute-start.28 = (bf16[56,48,128]{2,1,0:T(8,128)(2,1)}, bf16[56,48,128]{2,1,0:T(8,128)(2,1)}, u32[]{:S(2)}, u32[]{:S(2)}) collective-permute-start(bf16[56,48,128]{2,1,0:T(8,128)(2,1)} %get-tuple-element.54), channel_id=1, source_target_pairs={{0,13},{1,12},{2,15},{3,14},{4,9},{5,8},{6,11},{7,10}} | collective-permute-start | bytes 2064392 | tf_op jit(solution)/shard_map/ppermute | solution.py:322
  265.8 74.6 %collective-permute-start.29 = (bf16[56,48,128]{2,1,0:T(8,128)(2,1)}, bf16[56,48,128]{2,1,0:T(8,128)(2,1)}, u32[]{:S(2)}, u32[]{:S(2)}) collective-permute-start(bf16[56,48,128]{2,1,0:T(8,128)(2,1)} %get-tuple-element.55), channel_id=1, source_target_pairs={{0,14},{1,15},{2,12},{3,13},{4,10},{5,11},{6,8},{7,9}} | collective-permute-start | bytes 2064392 | tf_op jit(solution)/shard_map/ppermute | solution.py:322
  267.1 75.2 %collective-permute-start.30 = (bf16[56,48,128]{2,1,0:T(8,128)(2,1)}, bf16[56,48,128]{2,1,0:T(8,128)(2,1)}, u32[]{:S(2)}, u32[]{:S(2)}) collective-permute-start(bf16[56,48,128]{2,1,0:T(8,128)(2,1)} %get-tuple-element.56), channel_id=1, source_target_pairs={{0,15},{1,14},{2,13},{3,12},{4,11},{5,10},{6,9},{7,8}} | collective-permute-start | bytes 2064392 | tf_op jit(solution)/shard_map/ppermute | solution.py:322
  305.4 44.0 %collective-permute-start.19 = (bf16[49,48,128]{2,1,0:T(8,128)(2,1)}, bf16[49,48,128]{2,1,0:T(8,128)(2,1)S(1)}, u32[]{:S(2)}, u32[]{:S(2)}) collective-permute-start(bf16[49,48,128]{2,1,0:T(8,128)(2,1)} %get-tuple-element.45), channel_id=1, source_target_pairs={{8,10},{9,11},{10,8},{11,9},{12,14},{13,15},{14,12},{15,13}} | collective-permute-start | bytes 1806344 | tf_op jit(solution)/shard_map/ppermute | solution.py:322
  342.3 54.2 %collective-permute-start.22 = (bf16[49,48,128]{2,1,0:T(8,128)(2,1)}, bf16[49,48,128]{2,1,0:T(8,128)(2,1)S(1)}, u32[]{:S(2)}, u32[]{:S(2)}) collective-permute-start(bf16[49,48,128]{2,1,0:T(8,128)(2,1)} %get-tuple-element.48), channel_id=1, source_target_pairs={{8,13},{9,12},{10,15},{11,14},{12,9},{13,8},{14,11},{15,10}} | collective-permute-start | bytes 1806344 | tf_op jit(solution)/shard_map/ppermute | solution.py:322
  346.3 51.5 %collective-permute-start.23 = (bf16[49,48,128]{2,1,0:T(8,128)(2,1)}, bf16[49,48,128]{2,1,0:T(8,128)(2,1)S(1)}, u32[]{:S(2)}, u32[]{:S(2)}) collective-permute-start(bf16[49,48,128]{2,1,0:T(8,128)(2,1)} %get-tuple-element.49), channel_id=1, source_target_pairs={{8,14},{9,15},{10,12},{11,13},{12,10},{13,11},{14,8},{15,9}} | collective-permute-start | bytes 1806344 | tf_op jit(solution)/shard_map/ppermute | solution.py:322
  349.4 49.7 %collective-permute-start.24 = (bf16[49,48,128]{2,1,0:T(8,128)(2,1)}, bf16[49,48,128]{2,1,0:T(8,128)(2,1)S(1)}, u32[]{:S(2)}, u32[]{:S(2)}) collective-permute-start(bf16[49,48,128]{2,1,0:T(8,128)(2,1)} %get-tuple-element.50), channel_id=1, source_target_pairs={{8,15},{9,14},{10,13},{11,12},{12,11},{13,10},{14,9},{15,8}} | collective-permute-start | bytes 1806344 | tf_op jit(solution)/shard_map/ppermute | solution.py:322
  355.0 91.3 %collective-permute-start.2 = (bf16[14,48,128]{2,1,0:T(8,128)(2,1)S(1)}, bf16[14,48,128]{2,1,0:T(8,128)(2,1)S(1)}, u32[]{:S(2)}, u32[]{:S(2)}) collective-permute-start(bf16[14,48,128]{2,1,0:T(8,128)(2,1)S(1)} %slice.64), channel_id=1, source_target_pairs={{0,8},{1,9},{2,10},{3,11},{4,12},{5,13},{6,14},{7,15}} | collective-permute-start | bytes 516104 | tf_op jit(solution)/shard_map/ppermute | solution.py:322
  383.0 67.2 %collective-permute-start.31 = (bf16[6,48,128]{2,1,0:T(8,128)(2,1)S(1)}, bf16[6,48,128]{2,1,0:T(8,128)(2,1)S(1)}, u32[]{:S(2)}, u32[]{:S(2)}) collective-permute-start(bf16[6,48,128]{2,1,0:T(8,128)(2,1)S(1)} %get-tuple-element.67), channel_id=1, source_target_pairs={{0,8},{1,9},{2,10},{3,11},{4,12},{5,13},{6,14},{7,15}} | collective-permute-start | bytes 221192 | tf_op jit(solution)/shard_map/ppermute | solution.py:322
  396.5 53.7 %collective-permute-start.32 = (bf16[6,48,128]{2,1,0:T(8,128)(2,1)S(1)}, bf16[6,48,128]{2,1,0:T(8,128)(2,1)S(1)}, u32[]{:S(2)}, u32[]{:S(2)}) collective-permute-start(bf16[6,48,128]{2,1,0:T(8,128)(2,1)S(1)} %get-tuple-element.65), channel_id=1, source_target_pairs={{0,9},{1,8},{2,11},{3,10},{4,13},{5,12},{6,15},{7,14}} | collective-permute-start | bytes 221192 | tf_op jit(solution)/shard_map/ppermute | solution.py:322
  397.8 54.1 %collective-permute-start = (bf16[6,48,128]{2,1,0:T(8,128)(2,1)S(1)}, bf16[6,48,128]{2,1,0:T(8,128)(2,1)S(1)}, u32[]{:S(2)}, u32[]{:S(2)}) collective-permute-start(bf16[6,48,128]{2,1,0:T(8,128)(2,1)S(1)} %get-tuple-element.68), channel_id=1, source_target_pairs={{0,8},{1,9},{2,10},{3,11},{4,12},{5,13},{6,14},{7,15}} | collective-permute-start | bytes 221192 | tf_op jit(solution)/shard_map/ppermute | solution.py:322
  399.1 52.8 %collective-permute-start.1 = (bf16[6,48,128]{2,1,0:T(8,128)(2,1)S(1)}, bf16[6,48,128]{2,1,0:T(8,128)(2,1)S(1)}, u32[]{:S(2)}, u32[]{:S(2)}) collective-permute-start(bf16[6,48,128]{2,1,0:T(8,128)(2,1)S(1)} %get-tuple-element.66), channel_id=1, source_target_pairs={{0,9},{1,8},{2,11},{3,10},{4,13},{5,12},{6,15},{7,14}} | collective-permute-start | bytes 221192 | tf_op jit(solution)/shard_map/ppermute | solution.py:322
  (27 other events, 735.3 us)

commit v3 on v2

--- a/solution.py
+++ b/solution.py
@@ -21,9 +21,30 @@
 VMEM_LIMIT = 60 * 1024 * 1024
 PATCH_VMEM_LIMIT = 16 * 1024 * 1024
 HEAD = 2
-FETCHED = 2
+FETCHED = 3
 CROSS_CHUNKS = ((0, 16), (16, 12))
 LOCAL_CHUNKS = (((0, 28), (28, 28)), ((56, 16), (72, 14), (86, 6), (92, 6)))
+
+
+def head_body(x_ref, out, sem):
+    @pl.when(lax.axis_index("pp") == 0)
+    def _():
+        copy = pltpu.make_async_copy(x_ref.at[pl.ds(0, HEAD), :, pl.ds(0, RAW), :], out, sem)
+        copy.start()
+        copy.wait()
+
+
+def head_call(x_rows):
+    return pl.pallas_call(
+        head_body,
+        in_specs=[pl.BlockSpec(memory_space=pltpu.HBM)],
+        out_specs=pl.BlockSpec(memory_space=pltpu.VMEM),
+        out_shape=pltpu.VMEM((HEAD, COLS, RAW, CH), BF16),
+        scratch_shapes=[pltpu.SemaphoreType.DMA],
+        compiler_params=pltpu.CompilerParams(vmem_limit_bytes=PATCH_VMEM_LIMIT),
+        cost_estimate=pl.CostEstimate(flops=1000, bytes_accessed=HEAD * COLS * RAW * CH * 2, transcendentals=0),
+        name="head",
+    )(pltpu.with_memory_space_constraint(x_rows, pltpu.HBM))
 
 
 def conv_body(meta_ref, *refs, **sizes):
@@ -200,7 +221,7 @@
     )(meta, *operands)
 
 
-def patch_body(meta_ref, first, second, *refs, group0, steps, ahead, given):
+def patch_body(first, second, *refs, group0, steps, ahead, given):
     refs = list(refs)
     part_buf = refs.pop(0) if given else None
     before, result = refs.pop(0), refs.pop(0)
@@ -222,7 +243,7 @@
     def fetch(i):
         return pltpu.make_async_copy(before.at[pixels(ahead[0], i)], fetched.at[i], fetch_sem.at[i])
 
-    @pl.when(meta_ref[2] == 1)
+    @pl.when(lax.axis_index("pp") == 1)
     def _():
         if not given:
             arrivals = [pltpu.make_async_copy(ref, both_buf.at[k], both_sem.at[k]) for k, ref in enumerate((first, second))]
@@ -237,7 +258,7 @@
             for i in range(ahead[1]):
                 fetch(i).start()
 
-        begins = [3 * lax.bitwise_xor(meta_ref[0], k) + 1 for k in range(2)]
+        begins = [3 * lax.bitwise_xor(lax.axis_index("tp"), k) + 1 for k in range(2)]
         lane = lax.broadcasted_iota(jnp.int32, (16, LANES), 1)
         keep = []
         for tile in range(2):
@@ -279,13 +300,13 @@
                 fetch(i).wait()
 
 
-def patch_call(meta, first, second, result, group0, groups, ahead, part):
+def patch_call(first, second, result, group0, groups, ahead, part):
     assert group0 % 2 == 0 and groups % 2 == 0
     steps = groups // 2
     given = part is not None
     hbm, vmem = pl.BlockSpec(memory_space=pltpu.HBM), pl.BlockSpec(memory_space=pltpu.VMEM)
-    in_specs = [pl.BlockSpec(memory_space=pltpu.SMEM)] + ([vmem] * 3 if given else [hbm] * 2) + [hbm]
-    operands = [meta, first, second] + ([part] if given else []) + [result]
+    in_specs = ([vmem] * 3 if given else [hbm] * 2) + [hbm]
+    operands = [first, second] + ([part] if given else []) + [result]
     out_specs, out_shape = [hbm], [jax.ShapeDtypeStruct((ROWS * COLS, BLK, 192), BF16)]
     scratch = [pltpu.VMEM((steps, 16, BLK, 192), BF16), pltpu.SemaphoreType.DMA((steps,))]
     if not given:
@@ -322,7 +343,7 @@
             return lax.ppermute(value, ("pp", "tp"), pairs)
 
         x_rows = jnp.transpose(act_block, (1, 2, 0, 3))
-        raw_head = send(x_rows[:HEAD, :, :RAW], cross_pairs(0))
+        raw_head = send(head_call(x_rows), cross_pairs(0))
         raw_tail = send(x_rows[HEAD:, :, :RAW], cross_pairs(0))
         w_full = jnp.concatenate([lax.all_gather(w_shard[a], "tp", axis=1, tiled=True) for a in range(3)], axis=0)
         w_full = w_full.reshape(9 * CH, CH)
@@ -356,7 +377,7 @@
         parts = {}
         for n, (group0, groups, (first, second)) in enumerate(local_recv):
             ahead = local_recv[n + 2][:2] if n + 2 >= len(local_recv) - FETCHED and n + 2 < len(local_recv) else None
-            result = patch_call(r_meta, first, second, result, group0, groups, ahead, parts.get(n))
+            result = patch_call(first, second, result, group0, groups, ahead, parts.get(n))
             if ahead:
                 result, parts[n + 2] = result
         return jnp.transpose(result.reshape(ROWS, COLS, BLK, 192), (3, 0, 1, 2))

time: 455 us -> 451 us (level)
  transfers between devices with their start and end apart: 33 -> 33, of which waited for: 12 -> 12; matrix products, arithmetic and copies ran while one was open for 3% -> 3% of each run, Pallas kernels for 21% -> 20%
where the time goes in v3:
time: 451 us; the launch traced here: 449 us
  waiting for transfers between devices  229 us (51%)
  Pallas kernels  92.1 us (20%)
  starting transfers between devices  73.8 us (16%)
  blocking collectives  40.6 us (9%)
  local copies, waits for them, and re-layouts  10.2 us (2%)
    ppermute x33, waiting for transfers between devices, send(): return lax.ppermute(value, ('pp', 'tp'), pairs)  229 us
    ppermute x33, starting transfers between devices, send(): return lax.ppermute(value, ('pp', 'tp'), pairs)  73.8 us
    pallas_call x3, Pallas kernels, conv_call(): pl.pallas_call(functools.partial(conv_body, row0=row0, img0=img0, imgs=im...  43.1 us
    all_gather x3, blocking collectives, block_step(): lax.all_gather(w_shard[a], 'tp', axis=1, tiled=True)  31.2 us
    pallas_call x2, Pallas kernels, merge_call(): pl.pallas_call(functools.partial(merge_body, aliased=dst is not None), gr...  30.2 us
    pallas_call x6, Pallas kernels, patch_call(): pl.pallas_call(functools.partial(patch_body, group0=group0, steps=steps,...  18.8 us
    all_gather x1, blocking collectives, block_step(): lax.all_gather(jnp.stack([scale_shard, shift_shard]), 'tp', axis=1, tiled...  9.42 us
  transfers between devices with their start and end apart: 33, of which 12 were waited for; matrix products, arithmetic and copies ran while one was open for 3% of the time, Pallas kernels for 20%

profile of v3, /device:TPU:13, one launch (start us, length us, event | category | flops | bytes accessed | tf_op | source)
XLA Modules:
  0.0 449.4 jit_solution(15606945972636713744)
XLA Ops:
  1.5 4.8 %slice.74 = bf16[26,28,8,384]{3,2,1,0:T(8,128)(2,1)} slice(bf16[28,28,24,384]{3,2,1,0:T(8,128)(2,1)} %bitcast.23), slice={[2:28], [0:28], [0:8], [0:384]} | slice | bytes 8945664 | tf_op jit(solution)/shard_map/slice | solution.py:347
  7.6 9.4 %all-gather.3 = f32[8,48,2]{1,2,0:T(2,128)S(1)} all-gather(f32[1,48,2]{1,2,0:T(2,128)S(1)} %maximum_bitcast_fusion), channel_id=1, replica_groups=mesh['pp'=2,'tp'=8] {'tp'}, dimensions={0}, use_global_device_ids=true | all-gather | bytes 3456 | tf_op jit(solution)/shard_map/all_gather | solution.py:350
  17.8 10.1 %all-gather = bf16[1,3,384,384]{3,2,1,0:T(8,128)(2,1)S(1)} all-gather(bf16[1,3,48,384]{3,2,1,0:T(8,128)(2,1)S(1)} %get-tuple-element.73), channel_id=2, replica_groups=mesh['pp'=2,'tp'=8] {'tp'}, dimensions={2}, use_global_device_ids=true | all-gather | bytes 995328 | tf_op jit(solution)/shard_map/all_gather | solution.py:348
  27.8 11.0 %all-gather.2 = bf16[1,3,384,384]{3,2,1,0:T(8,128)(2,1)S(1)} all-gather(bf16[1,3,48,384]{3,2,1,0:T(8,128)(2,1)S(1)} %get-tuple-element.74), channel_id=4, replica_groups=mesh['pp'=2,'tp'=8] {'tp'}, dimensions={2}, use_global_device_ids=true | all-gather | bytes 995328 | tf_op jit(solution)/shard_map/all_gather | solution.py:348
  38.9 10.1 %all-gather.1 = bf16[1,3,384,384]{3,2,1,0:T(8,128)(2,1)S(1)} all-gather(bf16[1,3,48,384]{3,2,1,0:T(8,128)(2,1)S(1)} %get-tuple-element.75), channel_id=3, replica_groups=mesh['pp'=2,'tp'=8] {'tp'}, dimensions={2}, use_global_device_ids=true | all-gather | bytes 995328 | tf_op jit(solution)/shard_map/all_gather | solution.py:348
  51.4 4.0 shard_map.46
  55.4 4.2 shard_map.47
  66.5 64.9 %collective-permute-done.3.second = bf16[14,48,128]{2,1,0:T(8,128)(2,1)S(1)} collective-permute-done((bf16[14,48,128]{2,1,0:T(8,128)(2,1)S(1)}, bf16[14,48,128]{2,1,0:T(8,128)(2,1)S(1)}, u32[]{:S(2)}, u32[]{:S(2)}) %collective-permute-start.3) | collective-permute-done | bytes 172064 | tf_op jit(solution)/shard_map/ppermute | solution.py:343
  141.8 16.5 %collective-permute-done.7.second = bf16[28,48,128]{2,1,0:T(8,128)(2,1)S(1)} collective-permute-done((bf16[28,48,128]{2,1,0:T(8,128)(2,1)S(1)}, bf16[28,48,128]{2,1,0:T(8,128)(2,1)S(1)}, u32[]{:S(2)}, u32[]{:S(2)}) %collective-permute-start.7) | collective-permute-done | bytes 344096 | tf_op jit(solution)/shard_map/ppermute | solution.py:343
  159.5 16.8 %collective-permute-done.5.second = bf16[28,48,128]{2,1,0:T(8,128)(2,1)S(1)} collective-permute-done((bf16[28,48,128]{2,1,0:T(8,128)(2,1)S(1)}, bf16[28,48,128]{2,1,0:T(8,128)(2,1)S(1)}, u32[]{:S(2)}, u32[]{:S(2)}) %collective-permute-start.5) | collective-permute-done | bytes 344096 | tf_op jit(solution)/shard_map/ppermute | solution.py:343
  177.7 16.8 %collective-permute-done.6.first = bf16[28,48,128]{2,1,0:T(8,128)(2,1)S(1)} collective-permute-done((bf16[28,48,128]{2,1,0:T(8,128)(2,1)S(1)}, bf16[28,48,128]{2,1,0:T(8,128)(2,1)S(1)}, u32[]{:S(2)}, u32[]{:S(2)}) %collective-permute-start.6) | collective-permute-done | bytes 344096 | tf_op jit(solution)/shard_map/ppermute | solution.py:343
  195.7 9.5 %collective-permute-done.4.first = bf16[28,48,128]{2,1,0:T(8,128)(2,1)S(1)} collective-permute-done((bf16[28,48,128]{2,1,0:T(8,128)(2,1)S(1)}, bf16[28,48,128]{2,1,0:T(8,128)(2,1)S(1)}, u32[]{:S(2)}, u32[]{:S(2)}) %collective-permute-start.4) | collective-permute-done | bytes 344096 | tf_op jit(solution)/shard_map/ppermute | solution.py:343
  211.3 49.5 %collective-permute-done.11.refs_3_ = bf16[42,48,128]{2,1,0:T(8,128)(2,1)S(1)} collective-permute-done((bf16[42,48,128]{2,1,0:T(8,128)(2,1)}, bf16[42,48,128]{2,1,0:T(8,128)(2,1)S(1)}, u32[]{:S(2)}, u32[]{:S(2)}) %collective-permute-start.11) | collective-permute-done | bytes 516128 | tf_op jit(solution)/shard_map/ppermute | solution.py:343
  268.2 34.9 %shard_map.48 = (bf16[49,48,128]{2,1,0:T(8,128)(2,1)}, bf16[49,48,128]{2,1,0:T(8,128)(2,1)}, bf16[49,48,128]{2,1,0:T(8,128)(2,1)}, bf16[49,48,128]{2,1,0:T(8,128...) custom-call(s32[3]{0:T(128)} %pad_add_fusion.1.meta_ref, ...), custom_call_target="tpu_custom_call" | custom-call | flops 16647192576 | bytes 9633792 | tf_op jit(solution)/shard_map/pallas_call | solution.py:120
  305.1 19.9 %collective-permute-start.17 = (bf16[49,48,128]{2,1,0:T(8,128)(2,1)}, bf16[49,48,128]{2,1,0:T(8,128)(2,1)S(1)}, u32[]{:S(2)}, u32[]{:S(2)}) collective-permute-start(bf16[49,48,128]{2,1,0:T(8,128)(2,1)} %get-tuple-element.47), channel_id=1, source_target_pairs={{8,10},{9,11},{10,8},{11,9},{12,14},{13,15},{14,12},{15,13}} | collective-permute-start | bytes 1806344 | tf_op jit(solution)/shard_map/ppermute | solution.py:343
  325.0 9.0 %collective-permute-done.26.refs_3_ = bf16[56,48,128]{2,1,0:T(8,128)(2,1)} collective-permute-done((bf16[56,48,128]{2,1,0:T(8,128)(2,1)}, bf16[56,48,128]{2,1,0:T(8,128)(2,1)}, u32[]{:S(2)}, u32[]{:S(2)}) %collective-permute-start.26) | collective-permute-done | bytes 688160 | tf_op jit(solution)/shard_map/ppermute | solution.py:343
  334.0 6.0 %collective-permute-start.18 = (bf16[49,48,128]{2,1,0:T(8,128)(2,1)}, bf16[49,48,128]{2,1,0:T(8,128)(2,1)S(1)}, u32[]{:S(2)}, u32[]{:S(2)}) collective-permute-start(bf16[49,48,128]{2,1,0:T(8,128)(2,1)} %get-tuple-element.48), channel_id=1, source_target_pairs={{8,11},{9,10},{10,9},{11,8},{12,15},{13,14},{14,13},{15,12}} | collective-permute-start | bytes 1806344 | tf_op jit(solution)/shard_map/ppermute | solution.py:343
  342.0 3.9 collective-permute-start.20
  356.9 25.8 %collective-permute-done.19.refs_10_ = bf16[49,48,128]{2,1,0:T(8,128)(2,1)S(1)} collective-permute-done((bf16[49,48,128]{2,1,0:T(8,128)(2,1)}, bf16[49,48,128]{2,1,0:T(8,128)(2,1)S(1)}, u32[]{:S(2)}, u32[]{:S(2)}) %collective-permute-start.19) | collective-permute-done | bytes 602144 | tf_op jit(solution)/shard_map/ppermute | solution.py:343
  384.0 12.2 %collective-permute-done.20.refs_11_ = bf16[49,48,128]{2,1,0:T(8,128)(2,1)S(1)} collective-permute-done((bf16[49,48,128]{2,1,0:T(8,128)(2,1)}, bf16[49,48,128]{2,1,0:T(8,128)(2,1)S(1)}, u32[]{:S(2)}, u32[]{:S(2)}) %collective-permute-start.20) | collective-permute-done | bytes 602144 | tf_op jit(solution)/shard_map/ppermute | solution.py:343
  400.2 16.7 %shard_map.49.refs_14_ = bf16[784,48,192]{2,1,0:T(8,128)(2,1)} custom-call(s32[3]{0:T(128)} %pad_add_fusion.1.meta_ref, bf16[56,48,128]{2,1,0:T(8,128)(2,1)} %copy-done.8, bf16[56,48,128]{2,1,0:T(8,128)(2,1)} %copy-done.9, bf16[56,48,128]{2,1,0:T(8,128)(2,1)} %collective-permute-done.25.refs_2_, bf16[56,48,128]{2,1,0:T(8,128)(2,1)} %collective-permute-done.26.refs_3_, ...), custom_call_target="tpu_custom_call" | custom-call | flops 160000000 | bytes 16515072 | tf_op jit(solution)/shard_map/pallas_call | solution.py:208
  416.9 13.5 %shard_map.50.refs_0_ = bf16[784,48,192]{2,1,0:T(8,128)(2,1)} custom-call(s32[3]{0:T(128)} %pad_add_fusion.1.meta_ref, bf16[42,48,128]{2,1,0:T(8,128)(2,1)} %collective-permute-done.8.refs_0_, bf16[42,48,128]{2,1,0:T(8,128)(2,1)} %collective-permute-done.9.refs_1_, ...), custom_call_target="tpu_custom_call", output_to_operand_aliasing={{}: (15, {})} | custom-call | flops 120000000 | bytes 12386304 | tf_op jit(solution)/shard_map/pallas_call | solution.py:208
  430.4 5.2 %shard_map.51.refs_0_ = bf16[784,48,192]{2,1,0:T(8,128)(2,1)} custom-call(bf16[28,48,128]{2,1,0:T(8,128)(2,1)S(1)} %collective-permute-done.6.first, bf16[28,48,128]{2,1,0:T(8,128)(2,1)S(1)} %collective-permute-done.7.second, bf16[784,48,192]{2,1,0:T(8,128)(2,1)} %shard_map.50.refs_0_), custom_call_target="tpu_custom_call", output_to_operand_aliasing={{}: (2, {})} | custom-call | flops 28000000 | bytes 8257536 | tf_op jit(solution)/shard_map/pallas_call | solution.py:319
  435.6 5.9 %shard_map.52 = (bf16[784,48,192]{2,1,0:T(8,128)(2,1)}, bf16[7,16,48,192]{3,2,1,0:T(8,128)(2,1)S(1)}) custom-call(bf16[28,48,128]{2,1,0:T(8,128)(2,1)S(1)} %collective-permute-done.4.first, bf16[28,48,128]{2,1,0:T(8,128)(2,1)S(1)} %collective-permute-done.5.second, bf16[784,48,192]{2,1,0:T(8,128)(2,1)} %shard_map.51.refs_0_), custom_call_target="tpu_custom_call", output_to_operand_aliasing={{0}: (2, {})} | custom-call | flops 28000000 | bytes 8257536 | tf_op jit(solution)/shard_map/pallas_call | solution.py:319
  (107 shorter events, 67.8 us)
Async XLA Ops:
  0.1 140.4 %collective-permute-start.14 = (bf16[2,28,8,384]{3,2,1,0:T(8,128)(2,1)S(1)}, bf16[2,28,8,384]{3,2,1,0:T(8,128)(2,1)}, u32[]{:S(2)}, u32[]{:S(2)}) collective-permute-start(bf16[2,28,8,384]{3,2,1,0:T(8,128)(2,1)S(1)} %head.1), channel_id=1, source_target_pairs={{0,8},{1,9},{2,10},{3,11},{4,12},{5,13},{6,14},{7,15}} | collective-permute-start | bytes 1032200 | tf_op jit(solution)/shard_map/ppermute | solution.py:343
  6.3 260.5 %collective-permute-start.15 = (bf16[26,28,8,384]{3,2,1,0:T(8,128)(2,1)}, bf16[26,28,8,384]{3,2,1,0:T(8,128)(2,1)}, u32[]{:S(2)}, u32[]{:S(2)}) collective-permute-start(bf16[26,28,8,384]{3,2,1,0:T(8,128)(2,1)} %slice.74), channel_id=1, source_target_pairs={{0,8},{1,9},{2,10},{3,11},{4,12},{5,13},{6,14},{7,15}} | collective-permute-start | bytes 13418504 | tf_op jit(solution)/shard_map/ppermute | solution.py:343
  60.6 70.8 %collective-permute-start.3 = (bf16[14,48,128]{2,1,0:T(8,128)(2,1)S(1)}, bf16[14,48,128]{2,1,0:T(8,128)(2,1)S(1)}, u32[]{:S(2)}, u32[]{:S(2)}) collective-permute-start(bf16[14,48,128]{2,1,0:T(8,128)(2,1)S(1)} %slice.62), channel_id=1, source_target_pairs={{0,9},{1,8},{2,11},{3,10},{4,13},{5,12},{6,15},{7,14}} | collective-permute-start | bytes 516104 | tf_op jit(solution)/shard_map/ppermute | solution.py:343
  62.8 72.5 %collective-permute-start.30 = (bf16[16,48,128]{2,1,0:T(8,128)(2,1)S(1)}, bf16[16,48,128]{2,1,0:T(8,128)(2,1)S(1)}, u32[]{:S(2)}, u32[]{:S(2)}) collective-permute-start(bf16[16,48,128]{2,1,0:T(8,128)(2,1)S(1)} %slice.69), channel_id=1, source_target_pairs={{0,9},{1,8},{2,11},{3,10},{4,13},{5,12},{6,15},{7,14}} | collective-permute-start | bytes 589832 | tf_op jit(solution)/shard_map/ppermute | solution.py:343
  65.1 74.1 %collective-permute-start.29 = (bf16[16,48,128]{2,1,0:T(8,128)(2,1)S(1)}, bf16[16,48,128]{2,1,0:T(8,128)(2,1)S(1)}, u32[]{:S(2)}, u32[]{:S(2)}) collective-permute-start(bf16[16,48,128]{2,1,0:T(8,128)(2,1)S(1)} %slice.68), channel_id=1, source_target_pairs={{0,8},{1,9},{2,10},{3,11},{4,12},{5,13},{6,14},{7,15}} | collective-permute-start | bytes 589832 | tf_op jit(solution)/shard_map/ppermute | solution.py:343
  139.2 55.3 %collective-permute-start.6 = (bf16[28,48,128]{2,1,0:T(8,128)(2,1)S(1)}, bf16[28,48,128]{2,1,0:T(8,128)(2,1)S(1)}, u32[]{:S(2)}, u32[]{:S(2)}) collective-permute-start(bf16[28,48,128]{2,1,0:T(8,128)(2,1)S(1)} %get-tuple-element.67), channel_id=1, source_target_pairs={{0,8},{1,9},{2,10},{3,11},{4,12},{5,13},{6,14},{7,15}} | collective-permute-start | bytes 1032200 | tf_op jit(solution)/shard_map/ppermute | solution.py:343
  140.5 66.1 %collective-permute-start.8 = (bf16[42,48,128]{2,1,0:T(8,128)(2,1)}, bf16[42,48,128]{2,1,0:T(8,128)(2,1)}, u32[]{:S(2)}, u32[]{:S(2)}) collective-permute-start(bf16[42,48,128]{2,1,0:T(8,128)(2,1)} %get-tuple-element.39), channel_id=1, source_target_pairs={{0,10},{1,11},{2,8},{3,9},{4,14},{5,15},{6,12},{7,13}} | collective-permute-start | bytes 1548296 | tf_op jit(solution)/shard_map/ppermute | solution.py:343
  158.2 49.6 %collective-permute-start.9 = (bf16[42,48,128]{2,1,0:T(8,128)(2,1)}, bf16[42,48,128]{2,1,0:T(8,128)(2,1)}, u32[]{:S(2)}, u32[]{:S(2)}) collective-permute-start(bf16[42,48,128]{2,1,0:T(8,128)(2,1)} %get-tuple-element.40), channel_id=1, source_target_pairs={{0,11},{1,10},{2,9},{3,8},{4,15},{5,14},{6,13},{7,12}} | collective-permute-start | bytes 1548296 | tf_op jit(solution)/shard_map/ppermute | solution.py:343
  205.2 60.2 %collective-permute-start.23 = (bf16[56,48,128]{2,1,0:T(8,128)(2,1)}, bf16[56,48,128]{2,1,0:T(8,128)(2,1)S(1)}, u32[]{:S(2)}, u32[]{:S(2)}) collective-permute-start(bf16[56,48,128]{2,1,0:T(8,128)(2,1)} %get-tuple-element.53), channel_id=1, source_target_pairs={{0,10},{1,11},{2,8},{3,9},{4,14},{5,15},{6,12},{7,13}} | collective-permute-start | bytes 2064392 | tf_op jit(solution)/shard_map/ppermute | solution.py:343
  206.5 54.2 %collective-permute-start.11 = (bf16[42,48,128]{2,1,0:T(8,128)(2,1)}, bf16[42,48,128]{2,1,0:T(8,128)(2,1)S(1)}, u32[]{:S(2)}, u32[]{:S(2)}) collective-permute-start(bf16[42,48,128]{2,1,0:T(8,128)(2,1)} %get-tuple-element.42), channel_id=1, source_target_pairs={{0,13},{1,12},{2,15},{3,14},{4,9},{5,8},{6,11},{7,10}} | collective-permute-start | bytes 1548296 | tf_op jit(solution)/shard_map/ppermute | solution.py:343
  207.8 55.0 %collective-permute-start.12 = (bf16[42,48,128]{2,1,0:T(8,128)(2,1)}, bf16[42,48,128]{2,1,0:T(8,128)(2,1)}, u32[]{:S(2)}, u32[]{:S(2)}) collective-permute-start(bf16[42,48,128]{2,1,0:T(8,128)(2,1)} %get-tuple-element.43), channel_id=1, source_target_pairs={{0,14},{1,15},{2,12},{3,13},{4,10},{5,11},{6,8},{7,9}} | collective-permute-start | bytes 1548296 | tf_op jit(solution)/shard_map/ppermute | solution.py:343
  209.2 55.0 %collective-permute-start.13 = (bf16[42,48,128]{2,1,0:T(8,128)(2,1)}, bf16[42,48,128]{2,1,0:T(8,128)(2,1)}, u32[]{:S(2)}, u32[]{:S(2)}) collective-permute-start(bf16[42,48,128]{2,1,0:T(8,128)(2,1)} %get-tuple-element.44), channel_id=1, source_target_pairs={{0,15},{1,14},{2,13},{3,12},{4,11},{5,10},{6,9},{7,8}} | collective-permute-start | bytes 1548296 | tf_op jit(solution)/shard_map/ppermute | solution.py:343
  264.2 69.8 %collective-permute-start.26 = (bf16[56,48,128]{2,1,0:T(8,128)(2,1)}, bf16[56,48,128]{2,1,0:T(8,128)(2,1)}, u32[]{:S(2)}, u32[]{:S(2)}) collective-permute-start(bf16[56,48,128]{2,1,0:T(8,128)(2,1)} %get-tuple-element.56), channel_id=1, source_target_pairs={{0,13},{1,12},{2,15},{3,14},{4,9},{5,8},{6,11},{7,10}} | collective-permute-start | bytes 2064392 | tf_op jit(solution)/shard_map/ppermute | solution.py:343
  265.5 74.6 %collective-permute-start.27 = (bf16[56,48,128]{2,1,0:T(8,128)(2,1)}, bf16[56,48,128]{2,1,0:T(8,128)(2,1)}, u32[]{:S(2)}, u32[]{:S(2)}) collective-permute-start(bf16[56,48,128]{2,1,0:T(8,128)(2,1)} %get-tuple-element.57), channel_id=1, source_target_pairs={{0,14},{1,15},{2,12},{3,13},{4,10},{5,11},{6,8},{7,9}} | collective-permute-start | bytes 2064392 | tf_op jit(solution)/shard_map/ppermute | solution.py:343
  266.8 75.2 %collective-permute-start.28 = (bf16[56,48,128]{2,1,0:T(8,128)(2,1)}, bf16[56,48,128]{2,1,0:T(8,128)(2,1)}, u32[]{:S(2)}, u32[]{:S(2)}) collective-permute-start(bf16[56,48,128]{2,1,0:T(8,128)(2,1)} %get-tuple-element.58), channel_id=1, source_target_pairs={{0,15},{1,14},{2,13},{3,12},{4,11},{5,10},{6,9},{7,8}} | collective-permute-start | bytes 2064392 | tf_op jit(solution)/shard_map/ppermute | solution.py:343
  305.1 44.0 %collective-permute-start.17 = (bf16[49,48,128]{2,1,0:T(8,128)(2,1)}, bf16[49,48,128]{2,1,0:T(8,128)(2,1)S(1)}, u32[]{:S(2)}, u32[]{:S(2)}) collective-permute-start(bf16[49,48,128]{2,1,0:T(8,128)(2,1)} %get-tuple-element.47), channel_id=1, source_target_pairs={{8,10},{9,11},{10,8},{11,9},{12,14},{13,15},{14,12},{15,13}} | collective-permute-start | bytes 1806344 | tf_op jit(solution)/shard_map/ppermute | solution.py:343
  342.0 54.2 %collective-permute-start.20 = (bf16[49,48,128]{2,1,0:T(8,128)(2,1)}, bf16[49,48,128]{2,1,0:T(8,128)(2,1)S(1)}, u32[]{:S(2)}, u32[]{:S(2)}) collective-permute-start(bf16[49,48,128]{2,1,0:T(8,128)(2,1)} %get-tuple-element.50), channel_id=1, source_target_pairs={{8,13},{9,12},{10,15},{11,14},{12,9},{13,8},{14,11},{15,10}} | collective-permute-start | bytes 1806344 | tf_op jit(solution)/shard_map/ppermute | solution.py:343
  346.0 51.5 %collective-permute-start.21 = (bf16[49,48,128]{2,1,0:T(8,128)(2,1)}, bf16[49,48,128]{2,1,0:T(8,128)(2,1)S(1)}, u32[]{:S(2)}, u32[]{:S(2)}) collective-permute-start(bf16[49,48,128]{2,1,0:T(8,128)(2,1)} %get-tuple-element.51), channel_id=1, source_target_pairs={{8,14},{9,15},{10,12},{11,13},{12,10},{13,11},{14,8},{15,9}} | collective-permute-start | bytes 1806344 | tf_op jit(solution)/shard_map/ppermute | solution.py:343
  349.1 49.7 %collective-permute-start.22 = (bf16[49,48,128]{2,1,0:T(8,128)(2,1)}, bf16[49,48,128]{2,1,0:T(8,128)(2,1)S(1)}, u32[]{:S(2)}, u32[]{:S(2)}) collective-permute-start(bf16[49,48,128]{2,1,0:T(8,128)(2,1)} %get-tuple-element.52), channel_id=1, source_target_pairs={{8,15},{9,14},{10,13},{11,12},{12,11},{13,10},{14,9},{15,8}} | collective-permute-start | bytes 1806344 | tf_op jit(solution)/shard_map/ppermute | solution.py:343
  354.7 90.3 %collective-permute-start.2 = (bf16[14,48,128]{2,1,0:T(8,128)(2,1)S(1)}, bf16[14,48,128]{2,1,0:T(8,128)(2,1)S(1)}, u32[]{:S(2)}, u32[]{:S(2)}) collective-permute-start(bf16[14,48,128]{2,1,0:T(8,128)(2,1)S(1)} %slice.61), channel_id=1, source_target_pairs={{0,8},{1,9},{2,10},{3,11},{4,12},{5,13},{6,14},{7,15}} | collective-permute-start | bytes 516104 | tf_op jit(solution)/shard_map/ppermute | solution.py:343
  382.7 64.2 %collective-permute-start.31 = (bf16[6,48,128]{2,1,0:T(8,128)(2,1)S(1)}, bf16[6,48,128]{2,1,0:T(8,128)(2,1)S(1)}, u32[]{:S(2)}, u32[]{:S(2)}) collective-permute-start(bf16[6,48,128]{2,1,0:T(8,128)(2,1)S(1)} %get-tuple-element.71), channel_id=1, source_target_pairs={{0,8},{1,9},{2,10},{3,11},{4,12},{5,13},{6,14},{7,15}} | collective-permute-start | bytes 221192 | tf_op jit(solution)/shard_map/ppermute | solution.py:343
  396.2 50.7 %collective-permute-start.32 = (bf16[6,48,128]{2,1,0:T(8,128)(2,1)S(1)}, bf16[6,48,128]{2,1,0:T(8,128)(2,1)S(1)}, u32[]{:S(2)}, u32[]{:S(2)}) collective-permute-start(bf16[6,48,128]{2,1,0:T(8,128)(2,1)S(1)} %get-tuple-element.69), channel_id=1, source_target_pairs={{0,9},{1,8},{2,11},{3,10},{4,13},{5,12},{6,15},{7,14}} | collective-permute-start | bytes 221192 | tf_op jit(solution)/shard_map/ppermute | solution.py:343
  397.5 50.6 %collective-permute-start = (bf16[6,48,128]{2,1,0:T(8,128)(2,1)S(1)}, bf16[6,48,128]{2,1,0:T(8,128)(2,1)S(1)}, u32[]{:S(2)}, u32[]{:S(2)}) collective-permute-start(bf16[6,48,128]{2,1,0:T(8,128)(2,1)S(1)} %get-tuple-element.72), channel_id=1, source_target_pairs={{0,8},{1,9},{2,10},{3,11},{4,12},{5,13},{6,14},{7,15}} | collective-permute-start | bytes 221192 | tf_op jit(solution)/shard_map/ppermute | solution.py:343
  398.8 49.2 %collective-permute-start.1 = (bf16[6,48,128]{2,1,0:T(8,128)(2,1)S(1)}, bf16[6,48,128]{2,1,0:T(8,128)(2,1)S(1)}, u32[]{:S(2)}, u32[]{:S(2)}) collective-permute-start(bf16[6,48,128]{2,1,0:T(8,128)(2,1)S(1)} %get-tuple-element.70), channel_id=1, source_target_pairs={{0,9},{1,8},{2,11},{3,10},{4,13},{5,12},{6,15},{7,14}} | collective-permute-start | bytes 221192 | tf_op jit(solution)/shard_map/ppermute | solution.py:343
  (25 other events, 655.5 us)

commit v4 on v3

--- a/solution.py
+++ b/solution.py
@@ -20,10 +20,10 @@
 LANES = 128
 VMEM_LIMIT = 60 * 1024 * 1024
 PATCH_VMEM_LIMIT = 16 * 1024 * 1024
-HEAD = 2
+HEAD = 3
 FETCHED = 3
 CROSS_CHUNKS = ((0, 16), (16, 12))
-LOCAL_CHUNKS = (((0, 28), (28, 28)), ((56, 16), (72, 14), (86, 6), (92, 6)))
+LOCAL_CHUNKS = (((0, 56),), ((56, 16), (72, 14), (86, 6), (92, 6)))
 
 
 def head_body(x_ref, out, sem):
@@ -333,6 +333,8 @@
     def cross_pairs(k):
         return [(t, 8 + (t ^ k)) for t in range(8)]
 
+    both_pairs = [(t, (t + 8) % 16) for t in range(16)]
+
     def late_pairs(k):
         return [(8 + t, 8 + (t ^ k)) for t in range(8)]
 
@@ -343,7 +345,7 @@
             return lax.ppermute(value, ("pp", "tp"), pairs)
 
         x_rows = jnp.transpose(act_block, (1, 2, 0, 3))
-        raw_head = send(head_call(x_rows), cross_pairs(0))
+        raw_head = send(head_call(x_rows), both_pairs)
         raw_tail = send(x_rows[HEAD:, :, :RAW], cross_pairs(0))
         w_full = jnp.concatenate([lax.all_gather(w_shard[a], "tp", axis=1, tiled=True) for a in range(3)], axis=0)
         w_full = w_full.reshape(9 * CH, CH)

time: 451 us -> 431 us (0.956)
  the two profiles are of different devices: /device:TPU:13 before, /device:TPU:9 now
where the time goes in v4:
time: 431 us; the launch traced here: 429 us
  waiting for transfers between devices  231 us (54%)
  Pallas kernels  90.7 us (21%)
  starting transfers between devices  51.4 us (12%)
  blocking collectives  42.7 us (10%)
  local copies, waits for them, and re-layouts  10.1 us (2%)
    ppermute x31, waiting for transfers between devices, send(): return lax.ppermute(value, ('pp', 'tp'), pairs)  231 us
    ppermute x31, starting transfers between devices, send(): return lax.ppermute(value, ('pp', 'tp'), pairs)  51.4 us
    pallas_call x3, Pallas kernels, conv_call(): pl.pallas_call(functools.partial(conv_body, row0=row0, img0=img0, imgs=im...  43 us
    all_gather x3, blocking collectives, block_step(): lax.all_gather(w_shard[a], 'tp', axis=1, tiled=True)  32.1 us
    pallas_call x2, Pallas kernels, merge_call(): pl.pallas_call(functools.partial(merge_body, aliased=dst is not None), gr...  30.2 us
    pallas_call x5, Pallas kernels, patch_call(): pl.pallas_call(functools.partial(patch_body, group0=group0, steps=steps,...  17.5 us
    all_gather x1, blocking collectives, block_step(): lax.all_gather(jnp.stack([scale_shard, shift_shard]), 'tp', axis=1, tiled...  10.6 us
  transfers between devices with their start and end apart: 31, of which 14 were waited for; matrix products, arithmetic and copies ran while one was open for 3% of the time, Pallas kernels for 21%

profile of v4, /device:TPU:9, one launch (start us, length us, event | category | flops | bytes accessed | tf_op | source)
XLA Modules:
  0.0 429.4 jit_solution(4494708385908906612)
XLA Ops:
  0.5 4.7 %slice.58 = bf16[25,28,8,384]{3,2,1,0:T(8,128)(2,1)} slice(bf16[28,28,24,384]{3,2,1,0:T(8,128)(2,1)} %bitcast.23), slice={[3:28], [0:28], [0:8], [0:384]} | slice | bytes 8601600 | tf_op jit(solution)/shard_map/slice | solution.py:349
  6.5 10.6 %all-gather.3 = f32[8,48,2]{1,2,0:T(2,128)S(1)} all-gather(f32[1,48,2]{1,2,0:T(2,128)S(1)} %maximum_bitcast_fusion), channel_id=1, replica_groups=mesh['pp'=2,'tp'=8] {'tp'}, dimensions={0}, use_global_device_ids=true | all-gather | bytes 3456 | tf_op jit(solution)/shard_map/all_gather | solution.py:352
  17.8 11.0 %all-gather = bf16[1,3,384,384]{3,2,1,0:T(8,128)(2,1)S(1)} all-gather(bf16[1,3,48,384]{3,2,1,0:T(8,128)(2,1)S(1)} %get-tuple-element.69), channel_id=2, replica_groups=mesh['pp'=2,'tp'=8] {'tp'}, dimensions={2}, use_global_device_ids=true | all-gather | bytes 995328 | tf_op jit(solution)/shard_map/all_gather | solution.py:350
  28.8 10.1 %all-gather.2 = bf16[1,3,384,384]{3,2,1,0:T(8,128)(2,1)S(1)} all-gather(bf16[1,3,48,384]{3,2,1,0:T(8,128)(2,1)S(1)} %get-tuple-element.70), channel_id=4, replica_groups=mesh['pp'=2,'tp'=8] {'tp'}, dimensions={2}, use_global_device_ids=true | all-gather | bytes 995328 | tf_op jit(solution)/shard_map/all_gather | solution.py:350
  38.9 11.0 %all-gather.1 = bf16[1,3,384,384]{3,2,1,0:T(8,128)(2,1)S(1)} all-gather(bf16[1,3,48,384]{3,2,1,0:T(8,128)(2,1)S(1)} %get-tuple-element.71), channel_id=3, replica_groups=mesh['pp'=2,'tp'=8] {'tp'}, dimensions={2}, use_global_device_ids=true | all-gather | bytes 995328 | tf_op jit(solution)/shard_map/all_gather | solution.py:350
  52.4 4.1 shard_map.46
  56.4 4.1 shard_map.47
  67.3 75.2 %collective-permute-done.3.second = bf16[14,48,128]{2,1,0:T(8,128)(2,1)S(1)} collective-permute-done((bf16[14,48,128]{2,1,0:T(8,128)(2,1)S(1)}, bf16[14,48,128]{2,1,0:T(8,128)(2,1)S(1)}, u32[]{:S(2)}, u32[]{:S(2)}) %collective-permute-start.3) | collective-permute-done | bytes 172064 | tf_op jit(solution)/shard_map/ppermute | solution.py:345
  147.4 3.7 collective-permute-done.27.first
  155.0 14.1 %collective-permute-done.7.refs_1_ = bf16[42,48,128]{2,1,0:T(8,128)(2,1)S(1)} collective-permute-done((bf16[42,48,128]{2,1,0:T(8,128)(2,1)}, bf16[42,48,128]{2,1,0:T(8,128)(2,1)S(1)}, u32[]{:S(2)}, u32[]{:S(2)}) %collective-permute-start.7) | collective-permute-done | bytes 516128 | tf_op jit(solution)/shard_map/ppermute | solution.py:345
  170.4 13.8 %collective-permute-done.8.refs_2_ = bf16[42,48,128]{2,1,0:T(8,128)(2,1)S(1)} collective-permute-done((bf16[42,48,128]{2,1,0:T(8,128)(2,1)}, bf16[42,48,128]{2,1,0:T(8,128)(2,1)S(1)}, u32[]{:S(2)}, u32[]{:S(2)}) %collective-permute-start.8) | collective-permute-done | bytes 516128 | tf_op jit(solution)/shard_map/ppermute | solution.py:345
  185.5 16.9 %collective-permute-done.9.refs_3_ = bf16[42,48,128]{2,1,0:T(8,128)(2,1)S(1)} collective-permute-done((bf16[42,48,128]{2,1,0:T(8,128)(2,1)}, bf16[42,48,128]{2,1,0:T(8,128)(2,1)S(1)}, u32[]{:S(2)}, u32[]{:S(2)}) %collective-permute-start.9) | collective-permute-done | bytes 516128 | tf_op jit(solution)/shard_map/ppermute | solution.py:345
  206.4 30.3 %collective-permute-done.11.refs_5_ = bf16[42,48,128]{2,1,0:T(8,128)(2,1)} collective-permute-done((bf16[42,48,128]{2,1,0:T(8,128)(2,1)}, bf16[42,48,128]{2,1,0:T(8,128)(2,1)}, u32[]{:S(2)}, u32[]{:S(2)}) %collective-permute-start.11) | collective-permute-done | bytes 516128 | tf_op jit(solution)/shard_map/ppermute | solution.py:345
  238.0 13.5 %collective-permute-done.5.second = bf16[56,48,128]{2,1,0:T(8,128)(2,1)S(1)} collective-permute-done((bf16[56,48,128]{2,1,0:T(8,128)(2,1)}, bf16[56,48,128]{2,1,0:T(8,128)(2,1)S(1)}, u32[]{:S(2)}, u32[]{:S(2)}) %collective-permute-start.5) | collective-permute-done | bytes 688160 | tf_op jit(solution)/shard_map/ppermute | solution.py:345
  257.0 34.8 %shard_map.48 = (bf16[49,48,128]{2,1,0:T(8,128)(2,1)}, bf16[49,48,128]{2,1,0:T(8,128)(2,1)}, bf16[49,48,128]{2,1,0:T(8,128)(2,1)}, bf16[49,48,128]{2,1,0:T(8,128...) custom-call(s32[3]{0:T(128)} %pad_add_fusion.1.meta_ref, ...), custom_call_target="tpu_custom_call" | custom-call | flops 16647192576 | bytes 9633792 | tf_op jit(solution)/shard_map/pallas_call | solution.py:120
  291.9 8.8 %collective-permute-done.23.refs_2_ = bf16[56,48,128]{2,1,0:T(8,128)(2,1)} collective-permute-done((bf16[56,48,128]{2,1,0:T(8,128)(2,1)}, bf16[56,48,128]{2,1,0:T(8,128)(2,1)}, u32[]{:S(2)}, u32[]{:S(2)}) %collective-permute-start.23) | collective-permute-done | bytes 688160 | tf_op jit(solution)/shard_map/ppermute | solution.py:345
  300.7 4.1 collective-permute-start.14
  304.8 11.3 %collective-permute-done.24.refs_3_ = bf16[56,48,128]{2,1,0:T(8,128)(2,1)} collective-permute-done((bf16[56,48,128]{2,1,0:T(8,128)(2,1)}, bf16[56,48,128]{2,1,0:T(8,128)(2,1)}, u32[]{:S(2)}, u32[]{:S(2)}) %collective-permute-start.24) | collective-permute-done | bytes 688160 | tf_op jit(solution)/shard_map/ppermute | solution.py:345
  333.5 4.0 collective-permute-start.20
  337.5 9.5 %collective-permute-done.16.refs_9_ = bf16[49,48,128]{2,1,0:T(8,128)(2,1)S(1)} collective-permute-done((bf16[49,48,128]{2,1,0:T(8,128)(2,1)}, bf16[49,48,128]{2,1,0:T(8,128)(2,1)S(1)}, u32[]{:S(2)}, u32[]{:S(2)}) %collective-permute-start.16) | collective-permute-done | bytes 602144 | tf_op jit(solution)/shard_map/ppermute | solution.py:345
  350.5 27.0 %collective-permute-done.18.refs_11_ = bf16[49,48,128]{2,1,0:T(8,128)(2,1)S(1)} collective-permute-done((bf16[49,48,128]{2,1,0:T(8,128)(2,1)}, bf16[49,48,128]{2,1,0:T(8,128)(2,1)S(1)}, u32[]{:S(2)}, u32[]{:S(2)}) %collective-permute-start.18) | collective-permute-done | bytes 602144 | tf_op jit(solution)/shard_map/ppermute | solution.py:345
  381.5 16.7 %shard_map.49.refs_14_ = bf16[784,48,192]{2,1,0:T(8,128)(2,1)} custom-call(s32[3]{0:T(128)} %pad_add_fusion.1.meta_ref, bf16[56,48,128]{2,1,0:T(8,128)(2,1)} %copy-done.7, bf16[56,48,128]{2,1,0:T(8,128)(2,1)} %copy-done.8, bf16[56,48,128]{2,1,0:T(8,128)(2,1)} %collective-permute-done.23.refs_2_, bf16[56,48,128]{2,1,0:T(8,128)(2,1)} %collective-permute-done.24.refs_3_, ...), custom_call_target="tpu_custom_call" | custom-call | flops 160000000 | bytes 16515072 | tf_op jit(solution)/shard_map/pallas_call | solution.py:208
  398.3 13.5 %shard_map.50.refs_0_ = bf16[784,48,192]{2,1,0:T(8,128)(2,1)} custom-call(s32[3]{0:T(128)} %pad_add_fusion.1.meta_ref, bf16[42,48,128]{2,1,0:T(8,128)(2,1)} %copy-done.9, bf16[42,48,128]{2,1,0:T(8,128)(2,1)} %copy-done.10, bf16[42,48,128]{2,1,0:T(8,128)(2,1)} %copy-done.11, bf16[42,48,128]{2,1,0:T(8,128)(2,1)} %copy-done.12, ...), custom_call_target="tpu_custom_call", output_to_operand_aliasing={{}: (15, {})} | custom-call | flops 120000000 | bytes 12386304 | tf_op jit(solution)/shard_map/pallas_call | solution.py:208
  411.7 9.8 %shard_map.51 = (bf16[784,48,192]{2,1,0:T(8,128)(2,1)}, bf16[7,16,48,192]{3,2,1,0:T(8,128)(2,1)S(1)}) custom-call(bf16[56,48,128]{2,1,0:T(8,128)(2,1)S(1)} %collective-permute-done.4.first, bf16[56,48,128]{2,1,0:T(8,128)(2,1)S(1)} %collective-permute-done.5.second, bf16[784,48,192]{2,1,0:T(8,128)(2,1)} %shard_map.50.refs_0_), custom_call_target="tpu_custom_call", output_to_operand_aliasing={{0}: (2, {})} | custom-call | flops 56000000 | bytes 16515072 | tf_op jit(solution)/shard_map/pallas_call | solution.py:319
  (104 shorter events, 66.1 us)
Async XLA Ops:
  0.1 152.3 %collective-permute-start.12 = (bf16[3,28,8,384]{3,2,1,0:T(8,128)(2,1)S(1)}, bf16[3,28,8,384]{3,2,1,0:T(8,128)(2,1)}, u32[]{:S(2)}, u32[]{:S(2)}) collective-permute-start(bf16[3,28,8,384]{3,2,1,0:T(8,128)(2,1)S(1)} %head.1), channel_id=1, source_target_pairs={{0,8},{1,9},{2,10},{3,11},{4,12},{5,13},{6,14},{7,15},{8,0},{9,1},... | collective-permute-start | bytes 1548296 | tf_op jit(solution)/shard_map/ppermute | solution.py:345
  5.2 250.4 %collective-permute-start.13 = (bf16[25,28,8,384]{3,2,1,0:T(8,128)(2,1)}, bf16[25,28,8,384]{3,2,1,0:T(8,128)(2,1)}, u32[]{:S(2)}, u32[]{:S(2)}) collective-permute-start(bf16[25,28,8,384]{3,2,1,0:T(8,128)(2,1)} %slice.58), channel_id=1, source_target_pairs={{0,8},{1,9},{2,10},{3,11},{4,12},{5,13},{6,14},{7,15}} | collective-permute-start | bytes 12902408 | tf_op jit(solution)/shard_map/ppermute | solution.py:345
  61.5 81.0 %collective-permute-start.3 = (bf16[14,48,128]{2,1,0:T(8,128)(2,1)S(1)}, bf16[14,48,128]{2,1,0:T(8,128)(2,1)S(1)}, u32[]{:S(2)}, u32[]{:S(2)}) collective-permute-start(bf16[14,48,128]{2,1,0:T(8,128)(2,1)S(1)} %slice.50), channel_id=1, source_target_pairs={{0,9},{1,8},{2,11},{3,10},{4,13},{5,12},{6,15},{7,14}} | collective-permute-start | bytes 516104 | tf_op jit(solution)/shard_map/ppermute | solution.py:345
  62.8 90.9 %collective-permute-start.6 = (bf16[42,48,128]{2,1,0:T(8,128)(2,1)}, bf16[42,48,128]{2,1,0:T(8,128)(2,1)S(1)}, u32[]{:S(2)}, u32[]{:S(2)}) collective-permute-start(bf16[42,48,128]{2,1,0:T(8,128)(2,1)} %get-tuple-element.39), channel_id=1, source_target_pairs={{0,10},{1,11},{2,8},{3,9},{4,14},{5,15},{6,12},{7,13}} | collective-permute-start | bytes 1548296 | tf_op jit(solution)/shard_map/ppermute | solution.py:345
  65.0 81.0 %collective-permute-start.28 = (bf16[16,48,128]{2,1,0:T(8,128)(2,1)S(1)}, bf16[16,48,128]{2,1,0:T(8,128)(2,1)S(1)}, u32[]{:S(2)}, u32[]{:S(2)}) collective-permute-start(bf16[16,48,128]{2,1,0:T(8,128)(2,1)S(1)} %slice.53), channel_id=1, source_target_pairs={{0,9},{1,8},{2,11},{3,10},{4,13},{5,12},{6,15},{7,14}} | collective-permute-start | bytes 589832 | tf_op jit(solution)/shard_map/ppermute | solution.py:345
  151.1 33.1 %collective-permute-start.8 = (bf16[42,48,128]{2,1,0:T(8,128)(2,1)}, bf16[42,48,128]{2,1,0:T(8,128)(2,1)S(1)}, u32[]{:S(2)}, u32[]{:S(2)}) collective-permute-start(bf16[42,48,128]{2,1,0:T(8,128)(2,1)} %get-tuple-element.41), channel_id=1, source_target_pairs={{0,12},{1,13},{2,14},{3,15},{4,8},{5,9},{6,10},{7,11}} | collective-permute-start | bytes 1548296 | tf_op jit(solution)/shard_map/ppermute | solution.py:345
  152.4 50.0 %collective-permute-start.9 = (bf16[42,48,128]{2,1,0:T(8,128)(2,1)}, bf16[42,48,128]{2,1,0:T(8,128)(2,1)S(1)}, u32[]{:S(2)}, u32[]{:S(2)}) collective-permute-start(bf16[42,48,128]{2,1,0:T(8,128)(2,1)} %get-tuple-element.42), channel_id=1, source_target_pairs={{0,13},{1,12},{2,15},{3,14},{4,9},{5,8},{6,11},{7,10}} | collective-permute-start | bytes 1548296 | tf_op jit(solution)/shard_map/ppermute | solution.py:345
  153.7 50.0 %collective-permute-start.10 = (bf16[42,48,128]{2,1,0:T(8,128)(2,1)}, bf16[42,48,128]{2,1,0:T(8,128)(2,1)S(1)}, u32[]{:S(2)}, u32[]{:S(2)}) collective-permute-start(bf16[42,48,128]{2,1,0:T(8,128)(2,1)} %get-tuple-element.43), channel_id=1, source_target_pairs={{0,14},{1,15},{2,12},{3,13},{4,10},{5,11},{6,8},{7,9}} | collective-permute-start | bytes 1548296 | tf_op jit(solution)/shard_map/ppermute | solution.py:345
  169.1 82.4 %collective-permute-start.5 = (bf16[56,48,128]{2,1,0:T(8,128)(2,1)}, bf16[56,48,128]{2,1,0:T(8,128)(2,1)S(1)}, u32[]{:S(2)}, u32[]{:S(2)}) collective-permute-start(bf16[56,48,128]{2,1,0:T(8,128)(2,1)} %get-tuple-element.38), channel_id=1, source_target_pairs={{0,9},{1,8},{2,11},{3,10},{4,13},{5,12},{6,15},{7,14}} | collective-permute-start | bytes 2064392 | tf_op jit(solution)/shard_map/ppermute | solution.py:345
  184.2 68.6 %collective-permute-start.21 = (bf16[56,48,128]{2,1,0:T(8,128)(2,1)}, bf16[56,48,128]{2,1,0:T(8,128)(2,1)S(1)}, u32[]{:S(2)}, u32[]{:S(2)}) collective-permute-start(bf16[56,48,128]{2,1,0:T(8,128)(2,1)} %get-tuple-element.53), channel_id=1, source_target_pairs={{0,10},{1,11},{2,8},{3,9},{4,14},{5,15},{6,12},{7,13}} | collective-permute-start | bytes 2064392 | tf_op jit(solution)/shard_map/ppermute | solution.py:345
  202.4 51.8 %collective-permute-start.22 = (bf16[56,48,128]{2,1,0:T(8,128)(2,1)}, bf16[56,48,128]{2,1,0:T(8,128)(2,1)S(1)}, u32[]{:S(2)}, u32[]{:S(2)}) collective-permute-start(bf16[56,48,128]{2,1,0:T(8,128)(2,1)} %get-tuple-element.54), channel_id=1, source_target_pairs={{0,11},{1,10},{2,9},{3,8},{4,15},{5,14},{6,13},{7,12}} | collective-permute-start | bytes 2064392 | tf_op jit(solution)/shard_map/ppermute | solution.py:345
  236.7 88.5 %collective-permute-start.4 = (bf16[56,48,128]{2,1,0:T(8,128)(2,1)}, bf16[56,48,128]{2,1,0:T(8,128)(2,1)S(1)}, u32[]{:S(2)}, u32[]{:S(2)}) collective-permute-start(bf16[56,48,128]{2,1,0:T(8,128)(2,1)} %get-tuple-element.35.refs_7_), channel_id=1, source_target_pairs={{0,8},{1,9},{2,10},{3,11},{4,12},{5,13},{6,14},{7,15}} | collective-permute-start | bytes 2064392 | tf_op jit(solution)/shard_map/ppermute | solution.py:345
  251.5 49.2 %collective-permute-start.23 = (bf16[56,48,128]{2,1,0:T(8,128)(2,1)}, bf16[56,48,128]{2,1,0:T(8,128)(2,1)}, u32[]{:S(2)}, u32[]{:S(2)}) collective-permute-start(bf16[56,48,128]{2,1,0:T(8,128)(2,1)} %get-tuple-element.55), channel_id=1, source_target_pairs={{0,12},{1,13},{2,14},{3,15},{4,8},{5,9},{6,10},{7,11}} | collective-permute-start | bytes 2064392 | tf_op jit(solution)/shard_map/ppermute | solution.py:345
  252.8 63.3 %collective-permute-start.24 = (bf16[56,48,128]{2,1,0:T(8,128)(2,1)}, bf16[56,48,128]{2,1,0:T(8,128)(2,1)}, u32[]{:S(2)}, u32[]{:S(2)}) collective-permute-start(bf16[56,48,128]{2,1,0:T(8,128)(2,1)} %get-tuple-element.56), channel_id=1, source_target_pairs={{0,13},{1,12},{2,15},{3,14},{4,9},{5,8},{6,11},{7,10}} | collective-permute-start | bytes 2064392 | tf_op jit(solution)/shard_map/ppermute | solution.py:345
  254.3 63.9 %collective-permute-start.25 = (bf16[56,48,128]{2,1,0:T(8,128)(2,1)}, bf16[56,48,128]{2,1,0:T(8,128)(2,1)}, u32[]{:S(2)}, u32[]{:S(2)}) collective-permute-start(bf16[56,48,128]{2,1,0:T(8,128)(2,1)} %get-tuple-element.57), channel_id=1, source_target_pairs={{0,14},{1,15},{2,12},{3,13},{4,10},{5,11},{6,8},{7,9}} | collective-permute-start | bytes 2064392 | tf_op jit(solution)/shard_map/ppermute | solution.py:345
  255.6 65.8 %collective-permute-start.26 = (bf16[56,48,128]{2,1,0:T(8,128)(2,1)}, bf16[56,48,128]{2,1,0:T(8,128)(2,1)}, u32[]{:S(2)}, u32[]{:S(2)}) collective-permute-start(bf16[56,48,128]{2,1,0:T(8,128)(2,1)} %get-tuple-element.58), channel_id=1, source_target_pairs={{0,15},{1,14},{2,13},{3,12},{4,11},{5,10},{6,9},{7,8}} | collective-permute-start | bytes 2064392 | tf_op jit(solution)/shard_map/ppermute | solution.py:345
  325.2 52.3 %collective-permute-start.18 = (bf16[49,48,128]{2,1,0:T(8,128)(2,1)}, bf16[49,48,128]{2,1,0:T(8,128)(2,1)S(1)}, u32[]{:S(2)}, u32[]{:S(2)}) collective-permute-start(bf16[49,48,128]{2,1,0:T(8,128)(2,1)} %get-tuple-element.50), channel_id=1, source_target_pairs={{8,13},{9,12},{10,15},{11,14},{12,9},{13,8},{14,11},{15,10}} | collective-permute-start | bytes 1806344 | tf_op jit(solution)/shard_map/ppermute | solution.py:345
  327.7 51.1 %collective-permute-start.19 = (bf16[49,48,128]{2,1,0:T(8,128)(2,1)}, bf16[49,48,128]{2,1,0:T(8,128)(2,1)S(1)}, u32[]{:S(2)}, u32[]{:S(2)}) collective-permute-start(bf16[49,48,128]{2,1,0:T(8,128)(2,1)} %get-tuple-element.51), channel_id=1, source_target_pairs={{8,14},{9,15},{10,12},{11,13},{12,10},{13,11},{14,8},{15,9}} | collective-permute-start | bytes 1806344 | tf_op jit(solution)/shard_map/ppermute | solution.py:345
  333.5 46.6 %collective-permute-start.20 = (bf16[49,48,128]{2,1,0:T(8,128)(2,1)}, bf16[49,48,128]{2,1,0:T(8,128)(2,1)S(1)}, u32[]{:S(2)}, u32[]{:S(2)}) collective-permute-start(bf16[49,48,128]{2,1,0:T(8,128)(2,1)} %get-tuple-element.52), channel_id=1, source_target_pairs={{8,15},{9,14},{10,13},{11,12},{12,11},{13,10},{14,9},{15,8}} | collective-permute-start | bytes 1806344 | tf_op jit(solution)/shard_map/ppermute | solution.py:345
  347.0 78.0 %collective-permute-start.2 = (bf16[14,48,128]{2,1,0:T(8,128)(2,1)S(1)}, bf16[14,48,128]{2,1,0:T(8,128)(2,1)S(1)}, u32[]{:S(2)}, u32[]{:S(2)}) collective-permute-start(bf16[14,48,128]{2,1,0:T(8,128)(2,1)S(1)} %slice.49), channel_id=1, source_target_pairs={{0,8},{1,9},{2,10},{3,11},{4,12},{5,13},{6,14},{7,15}} | collective-permute-start | bytes 516104 | tf_op jit(solution)/shard_map/ppermute | solution.py:345
  349.2 77.6 %collective-permute-start.29 = (bf16[6,48,128]{2,1,0:T(8,128)(2,1)S(1)}, bf16[6,48,128]{2,1,0:T(8,128)(2,1)S(1)}, u32[]{:S(2)}, u32[]{:S(2)}) collective-permute-start(bf16[6,48,128]{2,1,0:T(8,128)(2,1)S(1)} %get-tuple-element.67), channel_id=1, source_target_pairs={{0,8},{1,9},{2,10},{3,11},{4,12},{5,13},{6,14},{7,15}} | collective-permute-start | bytes 221192 | tf_op jit(solution)/shard_map/ppermute | solution.py:345
  377.5 49.4 %collective-permute-start.30 = (bf16[6,48,128]{2,1,0:T(8,128)(2,1)S(1)}, bf16[6,48,128]{2,1,0:T(8,128)(2,1)S(1)}, u32[]{:S(2)}, u32[]{:S(2)}) collective-permute-start(bf16[6,48,128]{2,1,0:T(8,128)(2,1)S(1)} %get-tuple-element.65), channel_id=1, source_target_pairs={{0,9},{1,8},{2,11},{3,10},{4,13},{5,12},{6,15},{7,14}} | collective-permute-start | bytes 221192 | tf_op jit(solution)/shard_map/ppermute | solution.py:345
  378.8 49.2 %collective-permute-start = (bf16[6,48,128]{2,1,0:T(8,128)(2,1)S(1)}, bf16[6,48,128]{2,1,0:T(8,128)(2,1)S(1)}, u32[]{:S(2)}, u32[]{:S(2)}) collective-permute-start(bf16[6,48,128]{2,1,0:T(8,128)(2,1)S(1)} %get-tuple-element.68), channel_id=1, source_target_pairs={{0,8},{1,9},{2,10},{3,11},{4,12},{5,13},{6,14},{7,15}} | collective-permute-start | bytes 221192 | tf_op jit(solution)/shard_map/ppermute | solution.py:345
  380.2 47.9 %collective-permute-start.1 = (bf16[6,48,128]{2,1,0:T(8,128)(2,1)S(1)}, bf16[6,48,128]{2,1,0:T(8,128)(2,1)S(1)}, u32[]{:S(2)}, u32[]{:S(2)}) collective-permute-start(bf16[6,48,128]{2,1,0:T(8,128)(2,1)S(1)} %get-tuple-element.66), channel_id=1, source_target_pairs={{0,9},{1,8},{2,11},{3,10},{4,13},{5,12},{6,15},{7,14}} | collective-permute-start | bytes 221192 | tf_op jit(solution)/shard_map/ppermute | solution.py:345
  (25 other events, 596.8 us)
